TPU v7x, 32 devices: a whole 2x2x4 slice. The times are simulated.
32 devices in a mesh: dp: 2 (over x), expert: 16 (over z, y, core).
Axes of the slice: x: 2, y: 2, z: 4, core: 2. Of those that a mesh axis runs over, the one named last changes fastest.
Arguments:
- tokens: bfloat16 [256, 2048], P(('dp', 'expert')), may hold values from -6 to 6
- out_grad: bfloat16 [256, 2048], P(('dp', 'expert')), may hold values from -6 to 6
- expert_ids: int32 [256, 8], P(('dp', 'expert')), may hold values from 0 to 15, all different within a row; in each aligned block of 8 rows (0 to 7, 8 to 15, ...) at most 8 rows name the same one
- gate_values: float32 [256, 8], P(('dp', 'expert')), may hold values from 0.05 to 1
- w_gate: bfloat16 [16, 2048, 1024], P('expert', None, 'dp'), may hold values from -0.125 to 0.125
- w_up: bfloat16 [16, 2048, 1024], P('expert', None, 'dp'), may hold values from -0.125 to 0.125
- w_down: bfloat16 [16, 1024, 2048], P('expert', 'dp'), may hold values from -0.1875 to 0.1875
Outputs:
- grad_tokens: bfloat16 [256, 2048], P(('dp', 'expert'))
- grad_gate: float32 [16, 2048, 1024], P('expert', None, 'dp')
- grad_up: float32 [16, 2048, 1024], P('expert', None, 'dp')
- grad_down: float32 [16, 1024, 2048], P('expert', 'dp')
Inputs may be any that keep to these rules, and one draw needn't show every extreme that they name: `expert_ids`: each token names 8 different experts. Among the 8 tokens of one device (aligned blocks of 8 rows) no expert is named more than 8 times, and in every draw some expert is named exactly 8 times in some block.
All inputs are finite; a program needn't handle non-finite values.
Results may differ from a plain program's by a relative error of at most 0.014.
Values may be sent and summed in bfloat16 or wider, within the bound.
No kernel may reach another device: no remote copies, remote signals or barrier semaphores. Data moves between devices by JAX's collectives and lax.ppermute only.
A program may use at most 64 MiB of HBM per device.

v0:
```python
import functools

import jax
import jax.numpy as jnp
from jax import lax
from jax.experimental import pallas as pl
from jax.experimental.pallas import tpu as pltpu
from jax.sharding import PartitionSpec as P


AXES = ("dp", "expert")


def contract_last(left_op, right_op):
    return lax.dot_general(
        left_op, right_op, (((1,), (1,)), ((), ())), preferred_element_type=jnp.float32
    )


def contract_first(left_op, right_op):
    return lax.dot_general(
        left_op, right_op, (((0,), (0,)), ((), ())), preferred_element_type=jnp.float32
    )


def contract_inner(left_op, right_op):
    return jnp.dot(left_op, right_op, preferred_element_type=jnp.float32)


def hidden_grads(gate_pre, up_pre, act_grad):
    sigmoid_val = jax.nn.sigmoid(gate_pre)
    silu_val = gate_pre * sigmoid_val
    activation = (silu_val * up_pre).astype(jnp.bfloat16)
    up_grad = (act_grad * silu_val).astype(jnp.bfloat16)
    gate_grad = (act_grad * up_pre * sigmoid_val * (1.0 + gate_pre * (1.0 - sigmoid_val))).astype(
        jnp.bfloat16
    )
    return activation, gate_grad, up_grad


def swap(value, masks, device_count):
    even, odd = masks
    pairs = [(i, i ^ (odd if i % 2 else even)) for i in range(device_count)]
    return lax.ppermute(value, AXES, pairs)


def row_kernel(expert_count, tokens, out_grad, expert_ids, gate_values, rows, ids_held,
               values_held, copied):
    model_width = tokens.shape[1]
    gate_width = rows.shape[1] - 2 * model_width
    moves = (
        (expert_ids, ids_held),
        (gate_values, values_held),
        (tokens, rows.at[:, pl.ds(0, model_width)]),
        (out_grad, rows.at[:, pl.ds(model_width, model_width)]),
    )
    copies = [
        pltpu.make_async_copy(source, target, copied.at[i])
        for i, (source, target) in enumerate(moves)
    ]
    for copy in copies:
        copy.start()
    copies[0].wait()
    copies[1].wait()
    column = lax.broadcasted_iota(jnp.int32, (tokens.shape[0], gate_width), 1)
    expert = lax.rem(column, expert_count)
    ids, values = ids_held[...], values_held[...]
    weight = jnp.zeros(column.shape, jnp.float32)
    for k in range(ids.shape[1]):
        weight = weight + jnp.where(ids[:, k : k + 1] == expert, values[:, k : k + 1], 0.0)
    high = weight.astype(jnp.bfloat16).astype(jnp.float32)
    middle = (weight - high).astype(jnp.bfloat16).astype(jnp.float32)
    low = weight - high - middle
    place = lax.div(column, expert_count)
    piece = jnp.where(place == 0, high, jnp.where(place == 1, middle, low))
    piece = jnp.where(place < 3, piece, 0.0)
    rows[:, 2 * model_width :] = piece.astype(jnp.bfloat16)
    copies[2].wait()
    copies[3].wait()


def in_hbm(*values):
    return [pltpu.with_memory_space_constraint(value, pltpu.HBM) for value in values]


def routed_rows(tokens, out_grad, expert_ids, gate_values, expert_count):
    gate_width = -(-3 * expert_count // 128) * 128
    return pl.pallas_call(
        functools.partial(row_kernel, expert_count),
        out_shape=jax.ShapeDtypeStruct(
            (tokens.shape[0], 2 * tokens.shape[1] + gate_width), jnp.bfloat16
        ),
        in_specs=[pl.BlockSpec(memory_space=pltpu.HBM)] * 4,
        out_specs=pl.BlockSpec(memory_space=pltpu.VMEM),
        scratch_shapes=[
            pltpu.VMEM(expert_ids.shape, expert_ids.dtype),
            pltpu.VMEM(gate_values.shape, gate_values.dtype),
            pltpu.SemaphoreType.DMA((4,)),
        ],
        compiler_params=pltpu.CompilerParams(vmem_limit_bytes=4 << 20),
        name="routed_rows",
    )(*in_hbm(tokens, out_grad, expert_ids, gate_values))


def bring_kernel(count, *refs):
    sources, targets, copied = refs[:count], refs[count:-1], refs[-1]
    copies = [
        pltpu.make_async_copy(source, target, copied.at[i])
        for i, (source, target) in enumerate(zip(sources, targets))
    ]
    for copy in copies:
        copy.start()
    for copy in copies:
        copy.wait()


def bring(values):
    return pl.pallas_call(
        functools.partial(bring_kernel, len(values)),
        out_shape=[jax.ShapeDtypeStruct(value.shape, value.dtype) for value in values],
        in_specs=[pl.BlockSpec(memory_space=pltpu.HBM)] * len(values),
        out_specs=[pl.BlockSpec(memory_space=pltpu.VMEM)] * len(values),
        scratch_shapes=[pltpu.SemaphoreType.DMA((len(values),))],
        compiler_params=pltpu.CompilerParams(vmem_limit_bytes=8 << 20),
        name="bring",
    )(*in_hbm(*values))


def pass_kernel(expert_count, own_1, own_2, sib_1, sib_2, w_gate, w_up, w_down, *outs):
    activation, gate_grad, up_grad, g_rows, own_sums, sib_sums = outs
    model_width = w_gate.shape[0]
    half = own_1.shape[0]
    gate_width = own_1.shape[1] - 2 * model_width
    column = lax.broadcasted_iota(jnp.int32, (1, gate_width), 1)
    mine = (column < 3 * expert_count) & (
        lax.rem(column, expert_count) == lax.axis_index("expert")
    )
    for i, piece in enumerate((own_1, own_2, sib_1, sib_2)):
        pieces = piece[:, 2 * model_width :].astype(jnp.float32)
        gate = jnp.sum(jnp.where(mine, pieces, 0.0), axis=1, keepdims=True)
        grads = gate * piece[:, model_width : 2 * model_width].astype(jnp.float32)
        g_rows[i * half : (i + 1) * half, :] = grads.astype(jnp.bfloat16)
    x_rows = jnp.concatenate(
        [piece[:, :model_width] for piece in (own_1, own_2, sib_1, sib_2)], axis=0
    )
    act_value, gate_value, up_value = hidden_grads(
        contract_inner(x_rows, w_gate[...]),
        contract_inner(x_rows, w_up[...]),
        contract_last(g_rows[...], w_down[...]),
    )
    activation[...] = act_value
    gate_grad[...] = gate_value
    up_grad[...] = up_value
    sums = contract_last(gate_value, w_gate[...]) + contract_last(up_value, w_up[...])
    sums = sums.astype(jnp.bfloat16)
    quarter = half // 2
    for to, at in enumerate((0, 2, 1, 3)):
        own_sums[to * quarter : (to + 1) * quarter, :] = sums[at * quarter : (at + 1) * quarter]
        at = at + 4
        sib_sums[to * quarter : (to + 1) * quarter, :] = sums[at * quarter : (at + 1) * quarter]


def expert_pass(pieces, weights, expert_count):
    rows = 4 * pieces[0].shape[0]
    model_width, hidden_units = weights[0].shape
    hidden = jax.ShapeDtypeStruct((rows, hidden_units), jnp.bfloat16)
    wide = jax.ShapeDtypeStruct((rows, model_width), jnp.bfloat16)
    part = jax.ShapeDtypeStruct((rows // 2, model_width), jnp.bfloat16)
    in_vmem = pl.BlockSpec(memory_space=pltpu.VMEM)
    return pl.pallas_call(
        functools.partial(pass_kernel, expert_count),
        out_shape=(hidden, hidden, hidden, wide, part, part),
        in_specs=[in_vmem] * 7,
        out_specs=(in_vmem,) * 6,
        cost_estimate=pl.CostEstimate(
            flops=10 * rows * model_width * hidden_units,
            bytes_accessed=6 * model_width * hidden_units,
            transcendentals=rows * hidden_units,
        ),
        compiler_params=pltpu.CompilerParams(vmem_limit_bytes=24 << 20),
    )(*pieces, *weights)


def outer_kernel(left_count, right_count, steps, *refs):
    lefts, refs = refs[:left_count], refs[left_count:]
    each = (len(refs) - 2 * right_count - 1) // right_count
    rights, refs = refs[: each * right_count], refs[each * right_count :]
    outs, held, copied = refs[:right_count], refs[right_count:-1], refs[-1]
    width = outs[0].shape[0] // steps
    copies = []
    for step in range(steps):
        block = pl.ds(step * width, width)
        left = jnp.concatenate([value[:, block] for value in lefts], axis=0)
        for i in range(right_count):
            right = [value[...] for value in rights[i * each : (i + 1) * each]]
            held[i][block, :] = contract_first(left, jnp.concatenate(right, axis=0))
            copies.append(
                pltpu.make_async_copy(
                    held[i].at[block, :], outs[i].at[block, :], copied.at[len(copies)]
                )
            )
            copies[-1].start()
    for copy in copies:
        copy.wait()


def outer_sums(lefts, left_width, rights, steps):
    rows = sum(value.shape[0] for value in lefts)
    right_width = rights[0][0].shape[1]
    shape = (left_width, right_width)
    values = list(lefts) + [value for right in rights for value in right]
    return pl.pallas_call(
        functools.partial(outer_kernel, len(lefts), len(rights), steps),
        out_shape=[jax.ShapeDtypeStruct(shape, jnp.float32)] * len(rights),
        in_specs=[pl.BlockSpec(memory_space=pltpu.VMEM)] * len(values),
        out_specs=[pl.BlockSpec(memory_space=pltpu.HBM)] * len(rights),
        scratch_shapes=[pltpu.VMEM(shape, jnp.float32)] * len(rights)
        + [pltpu.SemaphoreType.DMA((steps * len(rights),))],
        cost_estimate=pl.CostEstimate(
            flops=2 * rows * left_width * right_width * len(rights),
            bytes_accessed=4 * left_width * right_width * len(rights),
            transcendentals=0,
        ),
        compiler_params=pltpu.CompilerParams(vmem_limit_bytes=24 << 20),
    )(*values)


def total(*values):
    return sum(value.astype(jnp.float32) for value in values).astype(jnp.bfloat16)


def add(left, right):
    return total(left, right)


def all_rows(tokens, out_grad, expert_ids, gate_values, w_gate, w_up, w_down):
    expert_count = lax.axis_size("expert")
    device_count = lax.axis_size("dp") * expert_count
    model_width, hidden_units = w_gate.shape[1:]
    top = device_count // 2
    side, cross, core = (2, top), (top, 2), (1, 1)
    both = (2 + top, 2 + top)
    line = top // 4

    def go(value, masks):
        return swap(value, masks, device_count)

    def along(value, step):
        return go(value, (4 * step, 4 * step))

    rows = routed_rows(tokens, out_grad, expert_ids, gate_values, expert_count)
    lines = [rows] + [along(rows, i) for i in range(1, line)]
    weights = bring((w_gate[0], w_up[0], w_down[0]))
    middle = line // 2
    early, early_sib, late = [], [], []
    for part in (lines[:middle], lines[middle:]):
        part = jnp.concatenate(part, axis=0)
        part = jnp.concatenate([part, go(part, side)], axis=0)
        early.append(part)
        late.append(go(part, cross))
        early_sib.append(go(part, core))
    early_out = expert_pass(early + early_sib, weights, expert_count)
    late, _ = lax.optimization_barrier((late, early_out[0]))
    late_sib = [go(part, core) for part in late]
    late_out = expert_pass(late + late_sib, weights, expert_count)
    half = early_out[4].shape[0] // 2
    early_sums = add(early_out[4], go(early_out[5], core))
    sided = go(early_sums[half:], side)
    late_sums = add(late_out[4], go(late_out[5], core))
    crossed = go(late_sums[:half], cross)
    returned = go(late_sums[half:], both)
    acts, gates, ups, g_rows = zip(early_out[:4], late_out[:4])
    pieces = early + early_sib + late + late_sib
    grad_gate, grad_up = outer_sums(pieces, model_width, (gates, ups), 8)
    crossed, grad_gate, grad_up = lax.optimization_barrier((crossed, grad_gate, grad_up))
    sums = total(early_sums[:half], sided, crossed, returned)
    parts = jnp.split(sums, line, axis=0)
    back = [along(parts[i], i) for i in range(1, line)]
    (grad_down,) = outer_sums(acts, hidden_units, (g_rows,), 4)
    return total(parts[0], *back), grad_gate[None], grad_up[None], grad_down[None]


def slot_table(expert_ids, gate_values, expert_count, capacity):
    tok_rows, top_count = expert_ids.shape
    flat_ids = expert_ids.reshape(-1)
    onehot = (flat_ids[:, None] == jnp.arange(expert_count, dtype=jnp.int32)[None, :]).astype(
        jnp.int32
    )
    before = jnp.cumsum(onehot, axis=0) - onehot
    slot_rank = jnp.sum(before * onehot, axis=1)
    slot_index = flat_ids * capacity + slot_rank
    slot_hits = (
        slot_index[:, None] == jnp.arange(expert_count * capacity, dtype=jnp.int32)[None, :]
    ).astype(jnp.float32)
    owner_row = jnp.arange(tok_rows * top_count, dtype=jnp.int32) // top_count
    token_hits = (owner_row[:, None] == jnp.arange(tok_rows, dtype=jnp.int32)[None, :]).astype(
        jnp.float32
    )
    weighted = slot_hits * gate_values.reshape(-1)[:, None]
    return jnp.dot(weighted.T, token_hits, precision=lax.Precision.HIGHEST)


def slot_rows(tokens, out_grad, expert_ids, gate_values, w_gate, w_up, w_down):
    expert_count = lax.axis_size("expert")
    _, model_width = tokens.shape
    capacity = slots_of(expert_ids.shape, expert_count)
    slot_count = expert_count * capacity
    gate_table = slot_table(expert_ids, gate_values, expert_count, capacity)
    pick_table = (gate_table > 0.0).astype(jnp.float32)

    def to_experts(rows):
        return lax.all_to_all(
            rows.reshape(expert_count, capacity, model_width),
            "expert",
            split_axis=0,
            concat_axis=0,
            tiled=True,
        ).reshape(slot_count, model_width)

    sent_rows = contract_inner(pick_table.astype(jnp.bfloat16), tokens).astype(jnp.bfloat16)
    sent_grads = jnp.dot(
        gate_table, out_grad.astype(jnp.float32), precision=lax.Precision.HIGHEST
    ).astype(jnp.bfloat16)
    x_rows = lax.all_gather(to_experts(sent_rows), "dp", axis=0, tiled=True)
    g_rows = lax.all_gather(to_experts(sent_grads), "dp", axis=0, tiled=True)
    activation, gate_grad, up_grad = hidden_grads(
        contract_inner(x_rows, w_gate[0]),
        contract_inner(x_rows, w_up[0]),
        contract_last(g_rows, w_down[0]),
    )
    sums = contract_last(gate_grad, w_gate[0]) + contract_last(up_grad, w_up[0])
    own_sums = lax.psum_scatter(
        sums.astype(jnp.bfloat16), "dp", scatter_dimension=0, tiled=True
    )
    back_rows = to_experts(own_sums).astype(jnp.float32)
    token_grad = jnp.dot(pick_table.T, back_rows, precision=lax.Precision.HIGHEST)
    grad_gate = contract_first(x_rows, gate_grad)
    grad_up = contract_first(x_rows, up_grad)
    grad_down = contract_first(activation, g_rows)
    return token_grad.astype(jnp.bfloat16), grad_gate[None], grad_up[None], grad_down[None]


def slots_of(ids_shape, expert_count):
    return 2 * ids_shape[0] * ids_shape[1] // expert_count


def solution(mesh):
    dp_count, expert_count = mesh.shape["dp"], mesh.shape["expert"]
    device_count = dp_count * expert_count

    def shards(tokens, out_grad, expert_ids, gate_values, w_gate, w_up, w_down):
        capacity = slots_of(expert_ids.shape, expert_count)
        paired = device_count >= 8 and device_count & (device_count - 1) == 0
        every_row = paired and expert_count * capacity >= expert_count * tokens.shape[0]
        body = all_rows if every_row else slot_rows
        return body(tokens, out_grad, expert_ids, gate_values, w_gate, w_up, w_down)

    split = P(AXES, None)
    return jax.shard_map(
        shards,
        mesh=mesh,
        in_specs=(split, split, split, split)
        + (P("expert", None, "dp"), P("expert", None, "dp"), P("expert", "dp", None)),
        out_specs=(split, P("expert", None, "dp"), P("expert", None, "dp"), P("expert", "dp", None)),
        check_vma=False,
    )
```

profile of v0, /device:TPU:0, one launch (start us, length us, event | category | flops | bytes accessed | tf_op | source)
XLA Modules:
  0.0 51.8 jit_solution(1278812895286034518)
XLA Ops:
  0.6 0.8 %routed_rows.1 = bf16[8,4224]{1,0:T(8,128)(2,1)S(1)} custom-call(bf16[8,2048]{1,0:T(8,128)(2,1)} %tokens.1, bf16[8,2048]{1,0:T(8,128)(2,1)} %out_grad.1, s32[8,8]{1,0:T(8,128)} %expert_ids.1, f32[8,8]{1,0:T(8,128)} %gate_values.1), custom_call_target="tpu_custom_call" | custom-call | tf_op jit(solution)/shard_map/routed_rows/pallas_call | solution.py:88
  1.5 3.1 %collective-permute-start = (bf16[8,4224]{1,0:T(8,128)(2,1)S(1)}, bf16[8,4224]{1,0:T(8,128)(2,1)S(1)}, u32[]{:S(2)}, u32[]{:S(2)}) collective-permute-start(bf16[8,4224]{1,0:T(8,128)(2,1)S(1)} %routed_rows.1), channel_id=1, source_target_pairs={{0,4},{1,5},{2,6},{3,7},{4,0},{5,1},{6,2},{7,3},{8,12},{9,13},{10,... | collective-permute-start | bytes 202760 | tf_op jit(solution)/shard_map/ppermute | solution.py:44
  4.6 2.6 %collective-permute-start.2 = (bf16[8,4224]{1,0:T(8,128)(2,1)S(1)}, bf16[8,4224]{1,0:T(8,128)(2,1)S(1)}, u32[]{:S(2)}, u32[]{:S(2)}) collective-permute-start(bf16[8,4224]{1,0:T(8,128)(2,1)S(1)} %routed_rows.1), channel_id=1, source_target_pairs={{0,8},{1,9},{2,10},{3,11},{4,12},{5,13},{6,14},{7,15},{8,0},{9,1},... | collective-permute-start | bytes 202760 | tf_op jit(solution)/shard_map/ppermute | solution.py:44
  7.2 1.8 %collective-permute-start.1 = (bf16[16,4224]{1,0:T(8,128)(2,1)S(1)}, bf16[16,4224]{1,0:T(8,128)(2,1)S(1)}, u32[]{:S(2)}, u32[]{:S(2)}) collective-permute-start(bf16[16,4224]{1,0:T(8,128)(2,1)S(1)} %pad_maximum_fusion.1), channel_id=1, source_target_pairs={{0,2},{1,17},{2,0},{3,19},{4,6},{5,21},{6,4},{7,23},{8,10},{9,25},... | collective-permute-start | bytes 405512 | tf_op jit(solution)/shard_map/ppermute | solution.py:44
  9.0 3.0 %collective-permute-done.2 = bf16[8,4224]{1,0:T(8,128)(2,1)S(1)} collective-permute-done((bf16[8,4224]{1,0:T(8,128)(2,1)S(1)}, bf16[8,4224]{1,0:T(8,128)(2,1)S(1)}, u32[]{:S(2)}, u32[]{:S(2)}) %collective-permute-start.2) | collective-permute-done | bytes 67616 | tf_op jit(solution)/shard_map/ppermute | solution.py:44
  12.0 1.4 %collective-permute-done.3 = bf16[8,4224]{1,0:T(8,128)(2,1)S(1)} collective-permute-done((bf16[8,4224]{1,0:T(8,128)(2,1)S(1)}, bf16[8,4224]{1,0:T(8,128)(2,1)S(1)}, u32[]{:S(2)}, u32[]{:S(2)}) %collective-permute-start.3) | collective-permute-done | bytes 67616 | tf_op jit(solution)/shard_map/ppermute | solution.py:44
  13.4 1.6 %collective-permute-start.4 = (bf16[16,4224]{1,0:T(8,128)(2,1)S(1)}, bf16[16,4224]{1,0:T(8,128)(2,1)S(1)}, u32[]{:S(2)}, u32[]{:S(2)}) collective-permute-start(bf16[16,4224]{1,0:T(8,128)(2,1)S(1)} %pad_maximum_fusion.2), channel_id=1, source_target_pairs={{0,2},{1,17},{2,0},{3,19},{4,6},{5,21},{6,4},{7,23},{8,10},{9,25},... | collective-permute-start | bytes 405512 | tf_op jit(solution)/shard_map/ppermute | solution.py:44
  15.1 3.4 %collective-permute-done.4 = bf16[16,4224]{1,0:T(8,128)(2,1)S(1)} collective-permute-done((bf16[16,4224]{1,0:T(8,128)(2,1)S(1)}, bf16[16,4224]{1,0:T(8,128)(2,1)S(1)}, u32[]{:S(2)}, u32[]{:S(2)}) %collective-permute-start.4) | collective-permute-done | bytes 135200 | tf_op jit(solution)/shard_map/ppermute | solution.py:44
  18.6 1.6 %collective-permute-start.9 = (bf16[32,4224]{1,0:T(8,128)(2,1)S(1)}, bf16[32,4224]{1,0:T(8,128)(2,1)S(1)}, u32[]{:S(2)}, u32[]{:S(2)}) collective-permute-start(bf16[32,4224]{1,0:T(8,128)(2,1)S(1)} %pad_maximum_fusion.own_1.refs_0_), channel_id=1, source_target_pairs={{0,16},{1,3},{2,18},{3,1},{4,20},{5,7},{6,22},{7,5},{8,24},{9,11},... | collective-permute-start | bytes 811016 | tf_op jit(solution)/shard_map/ppermute | solution.py:44
  20.7 2.9 %bring.1 = (bf16[2048,512]{1,0:T(8,128)(2,1)S(1)}, bf16[2048,512]{1,0:T(8,128)(2,1)S(1)}, bf16[512,2048]{1,0:T(8,128)(2,1)S(1)}) custom-call(bf16[2048,512]{1,0:T(8,128)(2,1)} %bitcast.7, bf16[2048,512]{1,0:T(8,128)(2,1)} %bitcast.8, bf16[512,2048]{1,0:T(8,128)(2,1)} %bitcast.9), custom_call_target="tpu_custom_call" | custom-call | tf_op jit(solution)/shard_map/bring/pallas_call | solution.py:118
  23.6 2.8 %shard_map.102 = (bf16[128,512]{1,0:T(8,128)(2,1)S(1)}, bf16[128,512]{1,0:T(8,128)(2,1)S(1)}, bf16[128,512]{1,0:T(8,128)(2,1)S(1)}, bf16[128,2048]{1,0:T(8,128)(...) custom-call(bf16[32,4224]{1,0:T(8,128)(2,1)S(1)} %pad_maximum_fusion.own_1.refs_0_, ...), custom_call_target="tpu_custom_call" | custom-call | flops 1342177280 | bytes 6291456 | tf_op jit(solution)/shard_map/pallas_call | solution.py:170
  26.4 1.6 %collective-permute-done.10.own_2.refs_5_ = bf16[32,4224]{1,0:T(8,128)(2,1)S(1)} collective-permute-done((bf16[32,4224]{1,0:T(8,128)(2,1)S(1)}, bf16[32,4224]{1,0:T(8,128)(2,1)S(1)}, u32[]{:S(2)}, u32[]{:S(2)}) %collective-permute-start.10) | collective-permute-done | bytes 270368 | tf_op jit(solution)/shard_map/ppermute | solution.py:44
  28.5 1.0 %collective-permute-done.11.sib_1.refs_6_ = bf16[32,4224]{1,0:T(8,128)(2,1)S(1)} collective-permute-done((bf16[32,4224]{1,0:T(8,128)(2,1)S(1)}, bf16[32,4224]{1,0:T(8,128)(2,1)S(1)}, u32[]{:S(2)}, u32[]{:S(2)}) %collective-permute-start.11) | collective-permute-done | bytes 270368 | tf_op jit(solution)/shard_map/ppermute | solution.py:44
  29.9 2.8 %shard_map.103 = (bf16[128,512]{1,0:T(8,128)(2,1)S(1)}, bf16[128,512]{1,0:T(8,128)(2,1)S(1)}, bf16[128,512]{1,0:T(8,128)(2,1)S(1)}, bf16[128,2048]{1,0:T(8,128)(...) custom-call(bf16[32,4224]{1,0:T(8,128)(2,1)S(1)} %collective-permute-done.9.own_1.refs_4_, ...), custom_call_target="tpu_custom_call" | custom-call | flops 1342177280 | bytes 6291456 | tf_op jit(solution)/shard_map/pallas_call | solution.py:170
  33.3 1.0 %collective-permute-done.13 = bf16[64,2048]{1,0:T(8,128)(2,1)S(1)} collective-permute-done((bf16[64,2048]{1,0:T(8,128)(2,1)S(1)}, bf16[64,2048]{1,0:T(8,128)(2,1)S(1)}, u32[]{:S(2)}, u32[]{:S(2)}) %collective-permute-start.13) | collective-permute-done | bytes 262176 | tf_op jit(solution)/shard_map/ppermute | solution.py:44
  34.4 1.6 %collective-permute-start.14 = (bf16[32,2048]{1,0:T(8,128)(2,1)S(1)}, bf16[32,2048]{1,0:T(8,128)(2,1)S(1)}, u32[]{:S(2)}, u32[]{:S(2)}) collective-permute-start(bf16[32,2048]{1,0:T(8,128)(2,1)S(1)} %get-tuple-element.48), channel_id=1, source_target_pairs={{0,16},{1,3},{2,18},{3,1},{4,20},{5,7},{6,22},{7,5},{8,24},{9,11},... | collective-permute-start | bytes 393224 | tf_op jit(solution)/shard_map/ppermute | solution.py:44
  36.1 1.6 %collective-permute-start.8 = (bf16[32,2048]{1,0:T(8,128)(2,1)S(1)}, bf16[32,2048]{1,0:T(8,128)(2,1)S(1)}, u32[]{:S(2)}, u32[]{:S(2)}) collective-permute-start(bf16[32,2048]{1,0:T(8,128)(2,1)S(1)} %slice.17), channel_id=1, source_target_pairs={{0,2},{1,17},{2,0},{3,19},{4,6},{5,21},{6,4},{7,23},{8,10},{9,25},... | collective-permute-start | bytes 393224 | tf_op jit(solution)/shard_map/ppermute | solution.py:44
  38.1 3.7 %shard_map.104 = (f32[2048,512]{1,0:T(8,128)}, f32[2048,512]{1,0:T(8,128)}) custom-call(bf16[32,4224]{1,0:T(8,128)(2,1)S(1)} %pad_maximum_fusion.own_1.refs_0_, bf16[32,4224]{1,0:T(8,128)(2,1)S(1)} %constant_dynamic-update-slice_fusion.own_2.refs_1_, bf16[32,4224]{1,0:T(8,128)(2,1)S(1)} %collective-permute-done.5.sib_1.refs_2_, ...), custom_call_target="tpu_custom_call" | custom-call | flops 1073741824 | bytes 8388608 | tf_op jit(solution)/shard_map/pallas_call | solution.py:212
  41.8 1.2 %collective-permute-done.8 = bf16[32,2048]{1,0:T(8,128)(2,1)S(1)} collective-permute-done((bf16[32,2048]{1,0:T(8,128)(2,1)S(1)}, bf16[32,2048]{1,0:T(8,128)(2,1)S(1)}, u32[]{:S(2)}, u32[]{:S(2)}) %collective-permute-start.8) | collective-permute-done | bytes 131104 | tf_op jit(solution)/shard_map/ppermute | solution.py:44
  43.0 1.2 %collective-permute-done.15 = bf16[32,2048]{1,0:T(8,128)(2,1)S(1)} collective-permute-done((bf16[32,2048]{1,0:T(8,128)(2,1)S(1)}, bf16[32,2048]{1,0:T(8,128)(2,1)S(1)}, u32[]{:S(2)}, u32[]{:S(2)}) %collective-permute-start.15) | collective-permute-done | bytes 131104 | tf_op jit(solution)/shard_map/ppermute | solution.py:44
  44.3 1.9 %collective-permute-start.18 = (bf16[8,2048]{1,0:T(8,128)(2,1)S(1)}, bf16[8,2048]{1,0:T(8,128)(2,1)S(1)}, u32[]{:S(2)}, u32[]{:S(2)}) collective-permute-start(bf16[8,2048]{1,0:T(8,128)(2,1)S(1)} %get-tuple-element.51), channel_id=1, source_target_pairs={{0,12},{1,13},{2,14},{3,15},{4,8},{5,9},{6,10},{7,11},{8,4},{9,5},... | collective-permute-start | bytes 98312 | tf_op jit(solution)/shard_map/ppermute | solution.py:44
  46.4 2.3 %collective-permute-start.16 = (bf16[8,2048]{1,0:T(8,128)(2,1)S(1)}, bf16[8,2048]{1,0:T(8,128)(2,1)S(1)}, u32[]{:S(2)}, u32[]{:S(2)}) collective-permute-start(bf16[8,2048]{1,0:T(8,128)(2,1)S(1)} %get-tuple-element.50), channel_id=1, source_target_pairs={{0,4},{1,5},{2,6},{3,7},{4,0},{5,1},{6,2},{7,3},{8,12},{9,13},{10,... | collective-permute-start | bytes 98312 | tf_op jit(solution)/shard_map/ppermute | solution.py:44
  48.7 2.4 %shard_map.105 = f32[512,2048]{1,0:T(8,128)} custom-call(bf16[128,512]{1,0:T(8,128)(2,1)S(1)} %get-tuple-element.31.refs_0_, bf16[128,512]{1,0:T(8,128)(2,1)S(1)} %get-tuple-element.45.refs_1_, bf16[128,2048]{1,0:T(8,128)(2,1)S(1)} %get-tuple-element.46.refs_2_, bf16[128,2048]{1,0:T(8,128)(2,1)S(1)} %get-tuple-element.47.refs_3_), custom_call_target="tpu_custom_call" | custom-call | flops 536870912 | bytes 4194304 | tf_op jit(solution)/shard_map/pallas_call | solution.py:212
  51.1 0.6 %add_convert_fusion.3 = bf16[8,2048]{1,0:T(8,128)(2,1)} fusion(bf16[8,2048]{1,0:T(8,128)(2,1)S(1)} %collective-permute-done.18, bf16[8,2048]{1,0:T(8,128)(2,1)S(1)} %collective-permute-done.17, bf16[8,2048]{1,0:T(8,128)(2,1)S(1)} %collective-permute-done.16, bf16[32,2048]{1,0:T(8,128)(2,1)S(1)} %add_convert_fusion.2), kind=kLoop, calls=%fused_computation.6 | loop fusion | flops 131072 | bytes 163840 | tf_op jit(solution)/shard_map/convert_element_type | solution.py:229
  (33 shorter events, 3.3 us)
Async XLA Ops:
  1.5 5.7 %collective-permute-start = (bf16[8,4224]{1,0:T(8,128)(2,1)S(1)}, bf16[8,4224]{1,0:T(8,128)(2,1)S(1)}, u32[]{:S(2)}, u32[]{:S(2)}) collective-permute-start(bf16[8,4224]{1,0:T(8,128)(2,1)S(1)} %routed_rows.1), channel_id=1, source_target_pairs={{0,4},{1,5},{2,6},{3,7},{4,0},{5,1},{6,2},{7,3},{8,12},{9,13},{10,... | collective-permute-start | bytes 202760 | tf_op jit(solution)/shard_map/ppermute | solution.py:44
  4.6 7.4 %collective-permute-start.2 = (bf16[8,4224]{1,0:T(8,128)(2,1)S(1)}, bf16[8,4224]{1,0:T(8,128)(2,1)S(1)}, u32[]{:S(2)}, u32[]{:S(2)}) collective-permute-start(bf16[8,4224]{1,0:T(8,128)(2,1)S(1)} %routed_rows.1), channel_id=1, source_target_pairs={{0,8},{1,9},{2,10},{3,11},{4,12},{5,13},{6,14},{7,15},{8,0},{9,1},... | collective-permute-start | bytes 202760 | tf_op jit(solution)/shard_map/ppermute | solution.py:44
  7.2 6.2 %collective-permute-start.3 = (bf16[8,4224]{1,0:T(8,128)(2,1)S(1)}, bf16[8,4224]{1,0:T(8,128)(2,1)S(1)}, u32[]{:S(2)}, u32[]{:S(2)}) collective-permute-start(bf16[8,4224]{1,0:T(8,128)(2,1)S(1)} %routed_rows.1), channel_id=1, source_target_pairs={{0,12},{1,13},{2,14},{3,15},{4,8},{5,9},{6,10},{7,11},{8,4},{9,5},... | collective-permute-start | bytes 202760 | tf_op jit(solution)/shard_map/ppermute | solution.py:44
  7.2 7.8 %collective-permute-start.1 = (bf16[16,4224]{1,0:T(8,128)(2,1)S(1)}, bf16[16,4224]{1,0:T(8,128)(2,1)S(1)}, u32[]{:S(2)}, u32[]{:S(2)}) collective-permute-start(bf16[16,4224]{1,0:T(8,128)(2,1)S(1)} %pad_maximum_fusion.1), channel_id=1, source_target_pairs={{0,2},{1,17},{2,0},{3,19},{4,6},{5,21},{6,4},{7,23},{8,10},{9,25},... | collective-permute-start | bytes 405512 | tf_op jit(solution)/shard_map/ppermute | solution.py:44
  13.4 5.1 %collective-permute-start.4 = (bf16[16,4224]{1,0:T(8,128)(2,1)S(1)}, bf16[16,4224]{1,0:T(8,128)(2,1)S(1)}, u32[]{:S(2)}, u32[]{:S(2)}) collective-permute-start(bf16[16,4224]{1,0:T(8,128)(2,1)S(1)} %pad_maximum_fusion.2), channel_id=1, source_target_pairs={{0,2},{1,17},{2,0},{3,19},{4,6},{5,21},{6,4},{7,23},{8,10},{9,25},... | collective-permute-start | bytes 405512 | tf_op jit(solution)/shard_map/ppermute | solution.py:44
  15.0 8.5 %collective-permute-start.5 = (bf16[32,4224]{1,0:T(8,128)(2,1)S(1)}, bf16[32,4224]{1,0:T(8,128)(2,1)S(1)}, u32[]{:S(2)}, u32[]{:S(2)}) collective-permute-start(bf16[32,4224]{1,0:T(8,128)(2,1)S(1)} %pad_maximum_fusion.own_1.refs_0_), channel_id=1, source_target_pairs={{0,1},{1,0},{2,3},{3,2},{4,5},{5,4},{6,7},{7,6},{8,9},{9,8},{10,11... | collective-permute-start | bytes 811016 | tf_op jit(solution)/shard_map/ppermute | solution.py:44
  18.5 5.1 %collective-permute-start.6 = (bf16[32,4224]{1,0:T(8,128)(2,1)S(1)}, bf16[32,4224]{1,0:T(8,128)(2,1)S(1)}, u32[]{:S(2)}, u32[]{:S(2)}) collective-permute-start(bf16[32,4224]{1,0:T(8,128)(2,1)S(1)} %constant_dynamic-update-slice_fusion.own_2.refs_1_), channel_id=1, source_target_pairs={{0,1},{1,0},{2,3},{3,2},{4,5},{5,4},{6,7},{7,6},{8,9},{9,8},{10,11... | collective-permute-start | bytes 811016 | tf_op jit(solution)/shard_map/ppermute | solution.py:44
  18.6 7.8 %collective-permute-start.9 = (bf16[32,4224]{1,0:T(8,128)(2,1)S(1)}, bf16[32,4224]{1,0:T(8,128)(2,1)S(1)}, u32[]{:S(2)}, u32[]{:S(2)}) collective-permute-start(bf16[32,4224]{1,0:T(8,128)(2,1)S(1)} %pad_maximum_fusion.own_1.refs_0_), channel_id=1, source_target_pairs={{0,16},{1,3},{2,18},{3,1},{4,20},{5,7},{6,22},{7,5},{8,24},{9,11},... | collective-permute-start | bytes 811016 | tf_op jit(solution)/shard_map/ppermute | solution.py:44
  20.1 7.9 %collective-permute-start.10 = (bf16[32,4224]{1,0:T(8,128)(2,1)S(1)}, bf16[32,4224]{1,0:T(8,128)(2,1)S(1)}, u32[]{:S(2)}, u32[]{:S(2)}) collective-permute-start(bf16[32,4224]{1,0:T(8,128)(2,1)S(1)} %constant_dynamic-update-slice_fusion.own_2.refs_1_), channel_id=1, source_target_pairs={{0,16},{1,3},{2,18},{3,1},{4,20},{5,7},{6,22},{7,5},{8,24},{9,11},... | collective-permute-start | bytes 811016 | tf_op jit(solution)/shard_map/ppermute | solution.py:44
  28.0 1.5 %collective-permute-start.11 = (bf16[32,4224]{1,0:T(8,128)(2,1)S(1)}, bf16[32,4224]{1,0:T(8,128)(2,1)S(1)}, u32[]{:S(2)}, u32[]{:S(2)}) collective-permute-start(bf16[32,4224]{1,0:T(8,128)(2,1)S(1)} %collective-permute-done.9.own_1.refs_4_), channel_id=1, source_target_pairs={{0,1},{1,0},{2,3},{3,2},{4,5},{5,4},{6,7},{7,6},{8,9},{9,8},{10,11... | collective-permute-start | bytes 811016 | tf_op jit(solution)/shard_map/ppermute | solution.py:44
  28.0 1.9 %collective-permute-start.12 = (bf16[32,4224]{1,0:T(8,128)(2,1)S(1)}, bf16[32,4224]{1,0:T(8,128)(2,1)S(1)}, u32[]{:S(2)}, u32[]{:S(2)}) collective-permute-start(bf16[32,4224]{1,0:T(8,128)(2,1)S(1)} %collective-permute-done.10.own_2.refs_5_), channel_id=1, source_target_pairs={{0,1},{1,0},{2,3},{3,2},{4,5},{5,4},{6,7},{7,6},{8,9},{9,8},{10,11... | collective-permute-start | bytes 811016 | tf_op jit(solution)/shard_map/ppermute | solution.py:44
  32.7 1.6 %collective-permute-start.13 = (bf16[64,2048]{1,0:T(8,128)(2,1)S(1)}, bf16[64,2048]{1,0:T(8,128)(2,1)S(1)}, u32[]{:S(2)}, u32[]{:S(2)}) collective-permute-start(bf16[64,2048]{1,0:T(8,128)(2,1)S(1)} %get-tuple-element.35), channel_id=1, source_target_pairs={{0,1},{1,0},{2,3},{3,2},{4,5},{5,4},{6,7},{7,6},{8,9},{9,8},{10,11... | collective-permute-start | bytes 786440 | tf_op jit(solution)/shard_map/ppermute | solution.py:44
  32.9 3.1 %collective-permute-start.7 = (bf16[64,2048]{1,0:T(8,128)(2,1)S(1)}, bf16[64,2048]{1,0:T(8,128)(2,1)S(1)}, u32[]{:S(2)}, u32[]{:S(2)}) collective-permute-start(bf16[64,2048]{1,0:T(8,128)(2,1)S(1)} %get-tuple-element.30), channel_id=1, source_target_pairs={{0,1},{1,0},{2,3},{3,2},{4,5},{5,4},{6,7},{7,6},{8,9},{9,8},{10,11... | collective-permute-start | bytes 786440 | tf_op jit(solution)/shard_map/ppermute | solution.py:44
  34.4 7.4 %collective-permute-start.14 = (bf16[32,2048]{1,0:T(8,128)(2,1)S(1)}, bf16[32,2048]{1,0:T(8,128)(2,1)S(1)}, u32[]{:S(2)}, u32[]{:S(2)}) collective-permute-start(bf16[32,2048]{1,0:T(8,128)(2,1)S(1)} %get-tuple-element.48), channel_id=1, source_target_pairs={{0,16},{1,3},{2,18},{3,1},{4,20},{5,7},{6,22},{7,5},{8,24},{9,11},... | collective-permute-start | bytes 393224 | tf_op jit(solution)/shard_map/ppermute | solution.py:44
  36.1 6.9 %collective-permute-start.8 = (bf16[32,2048]{1,0:T(8,128)(2,1)S(1)}, bf16[32,2048]{1,0:T(8,128)(2,1)S(1)}, u32[]{:S(2)}, u32[]{:S(2)}) collective-permute-start(bf16[32,2048]{1,0:T(8,128)(2,1)S(1)} %slice.17), channel_id=1, source_target_pairs={{0,2},{1,17},{2,0},{3,19},{4,6},{5,21},{6,4},{7,23},{8,10},{9,25},... | collective-permute-start | bytes 393224 | tf_op jit(solution)/shard_map/ppermute | solution.py:44
  37.7 6.5 %collective-permute-start.15 = (bf16[32,2048]{1,0:T(8,128)(2,1)S(1)}, bf16[32,2048]{1,0:T(8,128)(2,1)S(1)}, u32[]{:S(2)}, u32[]{:S(2)}) collective-permute-start(bf16[32,2048]{1,0:T(8,128)(2,1)S(1)} %get-tuple-element.49), channel_id=1, source_target_pairs={{0,18},{1,19},{2,16},{3,17},{4,22},{5,23},{6,20},{7,21},{8,26},{9,... | collective-permute-start | bytes 393224 | tf_op jit(solution)/shard_map/ppermute | solution.py:44
  44.3 6.8 %collective-permute-start.18 = (bf16[8,2048]{1,0:T(8,128)(2,1)S(1)}, bf16[8,2048]{1,0:T(8,128)(2,1)S(1)}, u32[]{:S(2)}, u32[]{:S(2)}) collective-permute-start(bf16[8,2048]{1,0:T(8,128)(2,1)S(1)} %get-tuple-element.51), channel_id=1, source_target_pairs={{0,12},{1,13},{2,14},{3,15},{4,8},{5,9},{6,10},{7,11},{8,4},{9,5},... | collective-permute-start | bytes 98312 | tf_op jit(solution)/shard_map/ppermute | solution.py:44
  46.2 5.0 %collective-permute-start.17 = (bf16[8,2048]{1,0:T(8,128)(2,1)S(1)}, bf16[8,2048]{1,0:T(8,128)(2,1)S(1)}, u32[]{:S(2)}, u32[]{:S(2)}) collective-permute-start(bf16[8,2048]{1,0:T(8,128)(2,1)S(1)} %get-tuple-element.52), channel_id=1, source_target_pairs={{0,8},{1,9},{2,10},{3,11},{4,12},{5,13},{6,14},{7,15},{8,0},{9,1},... | collective-permute-start | bytes 98312 | tf_op jit(solution)/shard_map/ppermute | solution.py:44
  46.4 4.7 %collective-permute-start.16 = (bf16[8,2048]{1,0:T(8,128)(2,1)S(1)}, bf16[8,2048]{1,0:T(8,128)(2,1)S(1)}, u32[]{:S(2)}, u32[]{:S(2)}) collective-permute-start(bf16[8,2048]{1,0:T(8,128)(2,1)S(1)} %get-tuple-element.50), channel_id=1, source_target_pairs={{0,4},{1,5},{2,6},{3,7},{4,0},{5,1},{6,2},{7,3},{8,12},{9,13},{10,... | collective-permute-start | bytes 98312 | tf_op jit(solution)/shard_map/ppermute | solution.py:44
where the time goes:
time: 52 us; the launch traced here: 51.8 us
  starting transfers between devices  20.5 us (39%)
  Pallas kernels  15.4 us (30%)
  waiting for transfers between devices  14.2 us (27%)
  other arithmetic  0.89 us (2%)
  between operations  0.79 us (2%)
    ppermute x19, starting transfers between devices, swap(): return lax.ppermute(value, AXES, pairs)  20.5 us
    ppermute x19, waiting for transfers between devices, swap(): return lax.ppermute(value, AXES, pairs)  14.2 us
    pallas_call x2, Pallas kernels, outer_sums(): pl.pallas_call(functools.partial(outer_kernel, len(lefts), len(rights), s...  6.04 us
    pallas_call x2, Pallas kernels, expert_pass(): pl.pallas_call(functools.partial(pass_kernel, expert_count), out_shape=(h...  5.6 us
    pallas_call x1, Pallas kernels, bring(): pl.pallas_call(functools.partial(bring_kernel, len(values)), out_shape=[j...  2.88 us
  transfers between devices with their start and end apart: 19, of which 9 were waited for; matrix products, arithmetic and copies ran while one was open for 0% of the time, Pallas kernels for 23%

commit v1 on v0

--- a/solution.py
+++ b/solution.py
@@ -114,6 +114,22 @@
         copy.wait()
 
 
+def column_kernel(expert_count, mine):
+    column = lax.broadcasted_iota(jnp.int32, mine.shape, 1)
+    own = lax.rem(column, expert_count) == lax.axis_index("expert")
+    mine[...] = jnp.where(own & (column < 3 * expert_count), 1.0, 0.0)
+
+
+def own_columns(expert_count, gate_width):
+    return pl.pallas_call(
+        functools.partial(column_kernel, expert_count),
+        out_shape=jax.ShapeDtypeStruct((1, gate_width), jnp.float32),
+        out_specs=pl.BlockSpec(memory_space=pltpu.VMEM),
+        compiler_params=pltpu.CompilerParams(vmem_limit_bytes=1 << 20),
+        name="own_columns",
+    )()
+
+
 def bring(values):
     return pl.pallas_call(
         functools.partial(bring_kernel, len(values)),
@@ -126,23 +142,22 @@
     )(*in_hbm(*values))
 
 
-def pass_kernel(expert_count, own_1, own_2, sib_1, sib_2, w_gate, w_up, w_down, *outs):
+def pass_kernel(piece_count, *refs):
+    pieces, (w_gate, w_up, w_down, mine), outs = (
+        refs[:piece_count],
+        refs[piece_count : piece_count + 4],
+        refs[piece_count + 4 :],
+    )
     activation, gate_grad, up_grad, g_rows, own_sums, sib_sums = outs
     model_width = w_gate.shape[0]
-    half = own_1.shape[0]
-    gate_width = own_1.shape[1] - 2 * model_width
-    column = lax.broadcasted_iota(jnp.int32, (1, gate_width), 1)
-    mine = (column < 3 * expert_count) & (
-        lax.rem(column, expert_count) == lax.axis_index("expert")
-    )
-    for i, piece in enumerate((own_1, own_2, sib_1, sib_2)):
-        pieces = piece[:, 2 * model_width :].astype(jnp.float32)
-        gate = jnp.sum(jnp.where(mine, pieces, 0.0), axis=1, keepdims=True)
+    row = 0
+    for piece in pieces:
+        weights = piece[:, 2 * model_width :].astype(jnp.float32)
+        gate = jnp.sum(weights * mine[...], axis=1, keepdims=True)
         grads = gate * piece[:, model_width : 2 * model_width].astype(jnp.float32)
-        g_rows[i * half : (i + 1) * half, :] = grads.astype(jnp.bfloat16)
-    x_rows = jnp.concatenate(
-        [piece[:, :model_width] for piece in (own_1, own_2, sib_1, sib_2)], axis=0
-    )
+        g_rows[row : row + piece.shape[0], :] = grads.astype(jnp.bfloat16)
+        row += piece.shape[0]
+    x_rows = jnp.concatenate([piece[:, :model_width] for piece in pieces], axis=0)
     act_value, gate_value, up_value = hidden_grads(
         contract_inner(x_rows, w_gate[...]),
         contract_inner(x_rows, w_up[...]),
@@ -152,25 +167,22 @@
     gate_grad[...] = gate_value
     up_grad[...] = up_value
     sums = contract_last(gate_value, w_gate[...]) + contract_last(up_value, w_up[...])
-    sums = sums.astype(jnp.bfloat16)
-    quarter = half // 2
-    for to, at in enumerate((0, 2, 1, 3)):
-        own_sums[to * quarter : (to + 1) * quarter, :] = sums[at * quarter : (at + 1) * quarter]
-        at = at + 4
-        sib_sums[to * quarter : (to + 1) * quarter, :] = sums[at * quarter : (at + 1) * quarter]
-
-
-def expert_pass(pieces, weights, expert_count):
-    rows = 4 * pieces[0].shape[0]
+    half = own_sums.shape[0]
+    own_sums[...] = sums[:half].astype(jnp.bfloat16)
+    sib_sums[...] = sums[half:].astype(jnp.bfloat16)
+
+
+def expert_pass(pieces, weights, mine):
+    rows = sum(piece.shape[0] for piece in pieces)
     model_width, hidden_units = weights[0].shape
     hidden = jax.ShapeDtypeStruct((rows, hidden_units), jnp.bfloat16)
     wide = jax.ShapeDtypeStruct((rows, model_width), jnp.bfloat16)
     part = jax.ShapeDtypeStruct((rows // 2, model_width), jnp.bfloat16)
     in_vmem = pl.BlockSpec(memory_space=pltpu.VMEM)
     return pl.pallas_call(
-        functools.partial(pass_kernel, expert_count),
+        functools.partial(pass_kernel, len(pieces)),
         out_shape=(hidden, hidden, hidden, wide, part, part),
-        in_specs=[in_vmem] * 7,
+        in_specs=[in_vmem] * (len(pieces) + 4),
         out_specs=(in_vmem,) * 6,
         cost_estimate=pl.CostEstimate(
             flops=10 * rows * model_width * hidden_units,
@@ -178,7 +190,7 @@
             transcendentals=rows * hidden_units,
         ),
         compiler_params=pltpu.CompilerParams(vmem_limit_bytes=24 << 20),
-    )(*pieces, *weights)
+    )(*pieces, *weights, mine)
 
 
 def outer_kernel(left_count, right_count, steps, *refs):
@@ -251,18 +263,20 @@
     rows = routed_rows(tokens, out_grad, expert_ids, gate_values, expert_count)
     lines = [rows] + [along(rows, i) for i in range(1, line)]
     weights = bring((w_gate[0], w_up[0], w_down[0]))
-    middle = line // 2
-    early, early_sib, late = [], [], []
-    for part in (lines[:middle], lines[middle:]):
-        part = jnp.concatenate(part, axis=0)
-        part = jnp.concatenate([part, go(part, side)], axis=0)
-        early.append(part)
-        late.append(go(part, cross))
-        early_sib.append(go(part, core))
-    early_out = expert_pass(early + early_sib, weights, expert_count)
+    mine = own_columns(expert_count, rows.shape[1] - 2 * model_width)
+    join = lambda *values: jnp.concatenate(values, axis=0)
+    rest = join(*lines[1:])
+    own = join(rows, rest)
+    own_side, rest_side = go(rows, side), go(rest, side)
+    early = [own, join(own_side, rest_side)]
+    crossing = (rows, rest, own_side, rest_side)
+    crossed = [go(part, cross) for part in crossing]
+    late = [join(*crossed[:2]), join(*crossed[2:])]
+    early_sib = [go(part, core) for part in early]
+    early_out = expert_pass(early + early_sib, weights, mine)
     late, _ = lax.optimization_barrier((late, early_out[0]))
     late_sib = [go(part, core) for part in late]
-    late_out = expert_pass(late + late_sib, weights, expert_count)
+    late_out = expert_pass(late + late_sib, weights, mine)
     half = early_out[4].shape[0] // 2
     early_sums = add(early_out[4], go(early_out[5], core))
     sided = go(early_sums[half:], side)

time: 52 us -> 54.6 us (1.050)
  starting transfers between devices: 20.5 us -> 22.6 us
    ppermute x19 -> x21, starting transfers between devices: 20.5 us -> 22.6 us  [swap(): return lax.ppermute(value, AXES, pairs)]
    ppermute x19 -> x21, waiting for transfers between devices: 14.2 us -> 14.6 us  [swap(): return lax.ppermute(value, AXES, pairs)]
    pallas_call x2 -> x3, Pallas kernels: 5.6 us -> 5.61 us  [the longest x2 5.6 us: expert_pass(): pl.pallas_call(functools.partial(pass_kernel, len(pieces)), out_shape=(hi...]
  transfers between devices with their start and end apart: 19 -> 21, of which waited for: 9 -> 7; matrix products, arithmetic and copies ran while one was open for 0% -> 1% of each run, Pallas kernels for 23% -> 16%
where the time goes in v1:
time: 54.6 us; the launch traced here: 54.4 us
  starting transfers between devices  22.6 us (41%)
  Pallas kernels  15.4 us (28%)
  waiting for transfers between devices  14.6 us (27%)
  other arithmetic  0.9 us (2%)
  between operations  0.86 us (2%)
    ppermute x21, starting transfers between devices, swap(): return lax.ppermute(value, AXES, pairs)  22.6 us
    ppermute x21, waiting for transfers between devices, swap(): return lax.ppermute(value, AXES, pairs)  14.6 us
    pallas_call x2, Pallas kernels, outer_sums(): pl.pallas_call(functools.partial(outer_kernel, len(lefts), len(rights), s...  6.05 us
    pallas_call x2, Pallas kernels, expert_pass(): pl.pallas_call(functools.partial(pass_kernel, len(pieces)), out_shape=(hi...  5.6 us
    pallas_call x1, Pallas kernels, bring(): pl.pallas_call(functools.partial(bring_kernel, len(values)), out_shape=[j...  2.88 us
  transfers between devices with their start and end apart: 21, of which 7 were waited for; matrix products, arithmetic and copies ran while one was open for 1% of the time, Pallas kernels for 16%

profile of v1, /device:TPU:0, one launch (start us, length us, event | category | flops | bytes accessed | tf_op | source)
XLA Modules:
  0.0 54.4 jit_solution(8402448447100475288)
XLA Ops:
  0.6 0.8 %routed_rows.1 = bf16[8,4224]{1,0:T(8,128)(2,1)S(1)} custom-call(bf16[8,2048]{1,0:T(8,128)(2,1)} %tokens.1, bf16[8,2048]{1,0:T(8,128)(2,1)} %out_grad.1, s32[8,8]{1,0:T(8,128)} %expert_ids.1, f32[8,8]{1,0:T(8,128)} %gate_values.1), custom_call_target="tpu_custom_call" | custom-call | tf_op jit(solution)/shard_map/routed_rows/pallas_call | solution.py:88
  1.5 3.1 %collective-permute-start = (bf16[8,4224]{1,0:T(8,128)(2,1)S(1)}, bf16[8,4224]{1,0:T(8,128)(2,1)S(1)}, u32[]{:S(2)}, u32[]{:S(2)}) collective-permute-start(bf16[8,4224]{1,0:T(8,128)(2,1)S(1)} %routed_rows.1), channel_id=1, source_target_pairs={{0,4},{1,5},{2,6},{3,7},{4,0},{5,1},{6,2},{7,3},{8,12},{9,13},{10,... | collective-permute-start | bytes 202760 | tf_op jit(solution)/shard_map/ppermute | solution.py:44
  4.6 2.6 %collective-permute-start.1 = (bf16[8,4224]{1,0:T(8,128)(2,1)S(1)}, bf16[8,4224]{1,0:T(8,128)(2,1)S(1)}, u32[]{:S(2)}, u32[]{:S(2)}) collective-permute-start(bf16[8,4224]{1,0:T(8,128)(2,1)S(1)} %routed_rows.1), channel_id=1, source_target_pairs={{0,8},{1,9},{2,10},{3,11},{4,12},{5,13},{6,14},{7,15},{8,0},{9,1},... | collective-permute-start | bytes 202760 | tf_op jit(solution)/shard_map/ppermute | solution.py:44
  7.2 1.7 %collective-permute-start.9 = (bf16[8,4224]{1,0:T(8,128)(2,1)S(1)}, bf16[8,4224]{1,0:T(8,128)(2,1)S(1)}, u32[]{:S(2)}, u32[]{:S(2)}) collective-permute-start(bf16[8,4224]{1,0:T(8,128)(2,1)S(1)} %routed_rows.1), channel_id=1, source_target_pairs={{0,16},{1,3},{2,18},{3,1},{4,20},{5,7},{6,22},{7,5},{8,24},{9,11},... | collective-permute-start | bytes 202760 | tf_op jit(solution)/shard_map/ppermute | solution.py:44
  8.9 1.5 %collective-permute-start.3 = (bf16[8,4224]{1,0:T(8,128)(2,1)S(1)}, bf16[8,4224]{1,0:T(8,128)(2,1)S(1)}, u32[]{:S(2)}, u32[]{:S(2)}) collective-permute-start(bf16[8,4224]{1,0:T(8,128)(2,1)S(1)} %routed_rows.1), channel_id=1, source_target_pairs={{0,2},{1,17},{2,0},{3,19},{4,6},{5,21},{6,4},{7,23},{8,10},{9,25},... | collective-permute-start | bytes 202760 | tf_op jit(solution)/shard_map/ppermute | solution.py:44
  10.4 2.9 %bring.1 = (bf16[2048,512]{1,0:T(8,128)(2,1)S(1)}, bf16[2048,512]{1,0:T(8,128)(2,1)S(1)}, bf16[512,2048]{1,0:T(8,128)(2,1)S(1)}) custom-call(bf16[2048,512]{1,0:T(8,128)(2,1)} %bitcast.7, bf16[2048,512]{1,0:T(8,128)(2,1)} %bitcast.8, bf16[512,2048]{1,0:T(8,128)(2,1)} %bitcast.9), custom_call_target="tpu_custom_call" | custom-call | tf_op jit(solution)/shard_map/bring/pallas_call | solution.py:134
  13.4 1.5 %collective-permute-start.10 = (bf16[24,4224]{1,0:T(8,128)(2,1)S(1)}, bf16[24,4224]{1,0:T(8,128)(2,1)S(1)}, u32[]{:S(2)}, u32[]{:S(2)}) collective-permute-start(bf16[24,4224]{1,0:T(8,128)(2,1)S(1)} %constant_dynamic-update-slice_fusion), channel_id=1, source_target_pairs={{0,16},{1,3},{2,18},{3,1},{4,20},{5,7},{6,22},{7,5},{8,24},{9,11},... | collective-permute-start | bytes 608264 | tf_op jit(solution)/shard_map/ppermute | solution.py:44
  14.9 1.5 %collective-permute-start.4 = (bf16[24,4224]{1,0:T(8,128)(2,1)S(1)}, bf16[24,4224]{1,0:T(8,128)(2,1)S(1)}, u32[]{:S(2)}, u32[]{:S(2)}) collective-permute-start(bf16[24,4224]{1,0:T(8,128)(2,1)S(1)} %constant_dynamic-update-slice_fusion), channel_id=1, source_target_pairs={{0,2},{1,17},{2,0},{3,19},{4,6},{5,21},{6,4},{7,23},{8,10},{9,25},... | collective-permute-start | bytes 608264 | tf_op jit(solution)/shard_map/ppermute | solution.py:44
  17.2 4.2 %collective-permute-done.4 = bf16[24,4224]{1,0:T(8,128)(2,1)S(1)} collective-permute-done((bf16[24,4224]{1,0:T(8,128)(2,1)S(1)}, bf16[24,4224]{1,0:T(8,128)(2,1)S(1)}, u32[]{:S(2)}, u32[]{:S(2)}) %collective-permute-start.4) | collective-permute-done | bytes 202784 | tf_op jit(solution)/shard_map/ppermute | solution.py:44
  21.5 0.6 %collective-permute-start.12 = (bf16[24,4224]{1,0:T(8,128)(2,1)S(1)}, bf16[24,4224]{1,0:T(8,128)(2,1)S(1)}, u32[]{:S(2)}, u32[]{:S(2)}) collective-permute-start(bf16[24,4224]{1,0:T(8,128)(2,1)S(1)} %collective-permute-done.4), channel_id=1, source_target_pairs={{0,16},{1,3},{2,18},{3,1},{4,20},{5,7},{6,22},{7,5},{8,24},{9,11},... | collective-permute-start | bytes 608264 | tf_op jit(solution)/shard_map/ppermute | solution.py:44
  22.2 5.1 %collective-permute-done.12 = bf16[24,4224]{1,0:T(8,128)(2,1)S(1)} collective-permute-done((bf16[24,4224]{1,0:T(8,128)(2,1)S(1)}, bf16[24,4224]{1,0:T(8,128)(2,1)S(1)}, u32[]{:S(2)}, u32[]{:S(2)}) %collective-permute-start.12) | collective-permute-done | bytes 202784 | tf_op jit(solution)/shard_map/ppermute | solution.py:44
  27.4 2.8 %shard_map.102 = (bf16[128,512]{1,0:T(8,128)(2,1)S(1)}, bf16[128,512]{1,0:T(8,128)(2,1)S(1)}, bf16[128,512]{1,0:T(8,128)(2,1)S(1)}, bf16[128,2048]{1,0:T(8,128)(...) custom-call(bf16[32,4224]{1,0:T(8,128)(2,1)S(1)} %pad_maximum_fusion.refs_0_, ...), custom_call_target="tpu_custom_call" | custom-call | flops 1342177280 | bytes 6291456 | tf_op jit(solution)/shard_map/pallas_call | solution.py:182
  30.7 1.0 %collective-permute-done.13.refs_2_.refs_6_ = bf16[32,4224]{1,0:T(8,128)(2,1)S(1)} collective-permute-done((bf16[32,4224]{1,0:T(8,128)(2,1)S(1)}, bf16[32,4224]{1,0:T(8,128)(2,1)S(1)}, u32[]{:S(2)}, u32[]{:S(2)}) %collective-permute-start.13) | collective-permute-done | bytes 270368 | tf_op jit(solution)/shard_map/ppermute | solution.py:44
  32.2 2.8 %shard_map.103 = (bf16[128,512]{1,0:T(8,128)(2,1)S(1)}, bf16[128,512]{1,0:T(8,128)(2,1)S(1)}, bf16[128,512]{1,0:T(8,128)(2,1)S(1)}, bf16[128,2048]{1,0:T(8,128)(...) custom-call(bf16[32,4224]{1,0:T(8,128)(2,1)S(1)} %pad_maximum_fusion.1.refs_0_.refs_4_, ...), custom_call_target="tpu_custom_call" | custom-call | flops 1342177280 | bytes 6291456 | tf_op jit(solution)/shard_map/pallas_call | solution.py:182
  35.5 1.0 %collective-permute-done.15 = bf16[64,2048]{1,0:T(8,128)(2,1)S(1)} collective-permute-done((bf16[64,2048]{1,0:T(8,128)(2,1)S(1)}, bf16[64,2048]{1,0:T(8,128)(2,1)S(1)}, u32[]{:S(2)}, u32[]{:S(2)}) %collective-permute-start.15) | collective-permute-done | bytes 262176 | tf_op jit(solution)/shard_map/ppermute | solution.py:44
  36.7 0.6 %collective-permute-start.16 = (bf16[32,2048]{1,0:T(8,128)(2,1)S(1)}, bf16[32,2048]{1,0:T(8,128)(2,1)S(1)}, u32[]{:S(2)}, u32[]{:S(2)}) collective-permute-start(bf16[32,2048]{1,0:T(8,128)(2,1)S(1)} %get-tuple-element.48), channel_id=1, source_target_pairs={{0,16},{1,3},{2,18},{3,1},{4,20},{5,7},{6,22},{7,5},{8,24},{9,11},... | collective-permute-start | bytes 393224 | tf_op jit(solution)/shard_map/ppermute | solution.py:44
  37.4 1.6 %collective-permute-start.8 = (bf16[32,2048]{1,0:T(8,128)(2,1)S(1)}, bf16[32,2048]{1,0:T(8,128)(2,1)S(1)}, u32[]{:S(2)}, u32[]{:S(2)}) collective-permute-start(bf16[32,2048]{1,0:T(8,128)(2,1)S(1)} %slice.17), channel_id=1, source_target_pairs={{0,2},{1,17},{2,0},{3,19},{4,6},{5,21},{6,4},{7,23},{8,10},{9,25},... | collective-permute-start | bytes 393224 | tf_op jit(solution)/shard_map/ppermute | solution.py:44
  38.9 1.4 %collective-permute-start.17 = (bf16[32,2048]{1,0:T(8,128)(2,1)S(1)}, bf16[32,2048]{1,0:T(8,128)(2,1)S(1)}, u32[]{:S(2)}, u32[]{:S(2)}) collective-permute-start(bf16[32,2048]{1,0:T(8,128)(2,1)S(1)} %get-tuple-element.49), channel_id=1, source_target_pairs={{0,18},{1,19},{2,16},{3,17},{4,22},{5,23},{6,20},{7,21},{8,26},{9,... | collective-permute-start | bytes 393224 | tf_op jit(solution)/shard_map/ppermute | solution.py:44
  40.4 3.7 %shard_map.104 = (f32[2048,512]{1,0:T(8,128)}, f32[2048,512]{1,0:T(8,128)}) custom-call(bf16[32,4224]{1,0:T(8,128)(2,1)S(1)} %pad_maximum_fusion.refs_0_, bf16[32,4224]{1,0:T(8,128)(2,1)S(1)} %constant_dynamic-update-slice_fusion.3.refs_1_, bf16[32,4224]{1,0:T(8,128)(2,1)S(1)} %collective-permute-done.5.refs_2_, ...), custom_call_target="tpu_custom_call" | custom-call | flops 1073741824 | bytes 8388608 | tf_op jit(solution)/shard_map/pallas_call | solution.py:224
  44.1 2.3 %collective-permute-done.17 = bf16[32,2048]{1,0:T(8,128)(2,1)S(1)} collective-permute-done((bf16[32,2048]{1,0:T(8,128)(2,1)S(1)}, bf16[32,2048]{1,0:T(8,128)(2,1)S(1)}, u32[]{:S(2)}, u32[]{:S(2)}) %collective-permute-start.17) | collective-permute-done | bytes 131104 | tf_op jit(solution)/shard_map/ppermute | solution.py:44
  46.5 2.5 %collective-permute-start.20 = (bf16[8,2048]{1,0:T(8,128)(2,1)S(1)}, bf16[8,2048]{1,0:T(8,128)(2,1)S(1)}, u32[]{:S(2)}, u32[]{:S(2)}) collective-permute-start(bf16[8,2048]{1,0:T(8,128)(2,1)S(1)} %get-tuple-element.51), channel_id=1, source_target_pairs={{0,12},{1,13},{2,14},{3,15},{4,8},{5,9},{6,10},{7,11},{8,4},{9,5},... | collective-permute-start | bytes 98312 | tf_op jit(solution)/shard_map/ppermute | solution.py:44
  49.0 2.0 %collective-permute-start.18 = (bf16[8,2048]{1,0:T(8,128)(2,1)S(1)}, bf16[8,2048]{1,0:T(8,128)(2,1)S(1)}, u32[]{:S(2)}, u32[]{:S(2)}) collective-permute-start(bf16[8,2048]{1,0:T(8,128)(2,1)S(1)} %get-tuple-element.50), channel_id=1, source_target_pairs={{0,4},{1,5},{2,6},{3,7},{4,0},{5,1},{6,2},{7,3},{8,12},{9,13},{10,... | collective-permute-start | bytes 98312 | tf_op jit(solution)/shard_map/ppermute | solution.py:44
  51.0 2.4 %shard_map.105 = f32[512,2048]{1,0:T(8,128)} custom-call(bf16[128,512]{1,0:T(8,128)(2,1)S(1)} %get-tuple-element.31.refs_0_, bf16[128,512]{1,0:T(8,128)(2,1)S(1)} %get-tuple-element.45.refs_1_, bf16[128,2048]{1,0:T(8,128)(2,1)S(1)} %get-tuple-element.46.refs_2_, bf16[128,2048]{1,0:T(8,128)(2,1)S(1)} %get-tuple-element.47.refs_3_), custom_call_target="tpu_custom_call" | custom-call | flops 536870912 | bytes 4194304 | tf_op jit(solution)/shard_map/pallas_call | solution.py:224
  53.8 0.6 %add_convert_fusion.3 = bf16[8,2048]{1,0:T(8,128)(2,1)} fusion(bf16[8,2048]{1,0:T(8,128)(2,1)S(1)} %collective-permute-done.20, bf16[8,2048]{1,0:T(8,128)(2,1)S(1)} %collective-permute-done.19, bf16[8,2048]{1,0:T(8,128)(2,1)S(1)} %collective-permute-done.18, bf16[32,2048]{1,0:T(8,128)(2,1)S(1)} %add_convert_fusion.2), kind=kLoop, calls=%fused_computation.6 | loop fusion | flops 131072 | bytes 163840 | tf_op jit(solution)/shard_map/convert_element_type | solution.py:241
  (40 shorter events, 3.1 us)
Async XLA Ops:
  1.5 11.8 %collective-permute-start = (bf16[8,4224]{1,0:T(8,128)(2,1)S(1)}, bf16[8,4224]{1,0:T(8,128)(2,1)S(1)}, u32[]{:S(2)}, u32[]{:S(2)}) collective-permute-start(bf16[8,4224]{1,0:T(8,128)(2,1)S(1)} %routed_rows.1), channel_id=1, source_target_pairs={{0,4},{1,5},{2,6},{3,7},{4,0},{5,1},{6,2},{7,3},{8,12},{9,13},{10,... | collective-permute-start | bytes 202760 | tf_op jit(solution)/shard_map/ppermute | solution.py:44
  4.6 8.7 %collective-permute-start.1 = (bf16[8,4224]{1,0:T(8,128)(2,1)S(1)}, bf16[8,4224]{1,0:T(8,128)(2,1)S(1)}, u32[]{:S(2)}, u32[]{:S(2)}) collective-permute-start(bf16[8,4224]{1,0:T(8,128)(2,1)S(1)} %routed_rows.1), channel_id=1, source_target_pairs={{0,8},{1,9},{2,10},{3,11},{4,12},{5,13},{6,14},{7,15},{8,0},{9,1},... | collective-permute-start | bytes 202760 | tf_op jit(solution)/shard_map/ppermute | solution.py:44
  7.2 6.2 %collective-permute-start.2 = (bf16[8,4224]{1,0:T(8,128)(2,1)S(1)}, bf16[8,4224]{1,0:T(8,128)(2,1)S(1)}, u32[]{:S(2)}, u32[]{:S(2)}) collective-permute-start(bf16[8,4224]{1,0:T(8,128)(2,1)S(1)} %routed_rows.1), channel_id=1, source_target_pairs={{0,12},{1,13},{2,14},{3,15},{4,8},{5,9},{6,10},{7,11},{8,4},{9,5},... | collective-permute-start | bytes 202760 | tf_op jit(solution)/shard_map/ppermute | solution.py:44
  7.2 14.3 %collective-permute-start.9 = (bf16[8,4224]{1,0:T(8,128)(2,1)S(1)}, bf16[8,4224]{1,0:T(8,128)(2,1)S(1)}, u32[]{:S(2)}, u32[]{:S(2)}) collective-permute-start(bf16[8,4224]{1,0:T(8,128)(2,1)S(1)} %routed_rows.1), channel_id=1, source_target_pairs={{0,16},{1,3},{2,18},{3,1},{4,20},{5,7},{6,22},{7,5},{8,24},{9,11},... | collective-permute-start | bytes 202760 | tf_op jit(solution)/shard_map/ppermute | solution.py:44
  8.9 7.7 %collective-permute-start.3 = (bf16[8,4224]{1,0:T(8,128)(2,1)S(1)}, bf16[8,4224]{1,0:T(8,128)(2,1)S(1)}, u32[]{:S(2)}, u32[]{:S(2)}) collective-permute-start(bf16[8,4224]{1,0:T(8,128)(2,1)S(1)} %routed_rows.1), channel_id=1, source_target_pairs={{0,2},{1,17},{2,0},{3,19},{4,6},{5,21},{6,4},{7,23},{8,10},{9,25},... | collective-permute-start | bytes 202760 | tf_op jit(solution)/shard_map/ppermute | solution.py:44
  13.4 8.7 %collective-permute-start.10 = (bf16[24,4224]{1,0:T(8,128)(2,1)S(1)}, bf16[24,4224]{1,0:T(8,128)(2,1)S(1)}, u32[]{:S(2)}, u32[]{:S(2)}) collective-permute-start(bf16[24,4224]{1,0:T(8,128)(2,1)S(1)} %constant_dynamic-update-slice_fusion), channel_id=1, source_target_pairs={{0,16},{1,3},{2,18},{3,1},{4,20},{5,7},{6,22},{7,5},{8,24},{9,11},... | collective-permute-start | bytes 608264 | tf_op jit(solution)/shard_map/ppermute | solution.py:44
  14.9 6.5 %collective-permute-start.4 = (bf16[24,4224]{1,0:T(8,128)(2,1)S(1)}, bf16[24,4224]{1,0:T(8,128)(2,1)S(1)}, u32[]{:S(2)}, u32[]{:S(2)}) collective-permute-start(bf16[24,4224]{1,0:T(8,128)(2,1)S(1)} %constant_dynamic-update-slice_fusion), channel_id=1, source_target_pairs={{0,2},{1,17},{2,0},{3,19},{4,6},{5,21},{6,4},{7,23},{8,10},{9,25},... | collective-permute-start | bytes 608264 | tf_op jit(solution)/shard_map/ppermute | solution.py:44
  16.5 10.8 %collective-permute-start.5 = (bf16[32,4224]{1,0:T(8,128)(2,1)S(1)}, bf16[32,4224]{1,0:T(8,128)(2,1)S(1)}, u32[]{:S(2)}, u32[]{:S(2)}) collective-permute-start(bf16[32,4224]{1,0:T(8,128)(2,1)S(1)} %pad_maximum_fusion.refs_0_), channel_id=1, source_target_pairs={{0,1},{1,0},{2,3},{3,2},{4,5},{5,4},{6,7},{7,6},{8,9},{9,8},{10,11... | collective-permute-start | bytes 811016 | tf_op jit(solution)/shard_map/ppermute | solution.py:44
  16.6 5.6 %collective-permute-start.11 = (bf16[8,4224]{1,0:T(8,128)(2,1)S(1)}, bf16[8,4224]{1,0:T(8,128)(2,1)S(1)}, u32[]{:S(2)}, u32[]{:S(2)}) collective-permute-start(bf16[8,4224]{1,0:T(8,128)(2,1)S(1)} %collective-permute-done.3), channel_id=1, source_target_pairs={{0,16},{1,3},{2,18},{3,1},{4,20},{5,7},{6,22},{7,5},{8,24},{9,11},... | collective-permute-start | bytes 202760 | tf_op jit(solution)/shard_map/ppermute | solution.py:44
  21.4 5.9 %collective-permute-start.6 = (bf16[32,4224]{1,0:T(8,128)(2,1)S(1)}, bf16[32,4224]{1,0:T(8,128)(2,1)S(1)}, u32[]{:S(2)}, u32[]{:S(2)}) collective-permute-start(bf16[32,4224]{1,0:T(8,128)(2,1)S(1)} %constant_dynamic-update-slice_fusion.3.refs_1_), channel_id=1, source_target_pairs={{0,1},{1,0},{2,3},{3,2},{4,5},{5,4},{6,7},{7,6},{8,9},{9,8},{10,11... | collective-permute-start | bytes 811016 | tf_op jit(solution)/shard_map/ppermute | solution.py:44
  21.5 5.8 %collective-permute-start.12 = (bf16[24,4224]{1,0:T(8,128)(2,1)S(1)}, bf16[24,4224]{1,0:T(8,128)(2,1)S(1)}, u32[]{:S(2)}, u32[]{:S(2)}) collective-permute-start(bf16[24,4224]{1,0:T(8,128)(2,1)S(1)} %collective-permute-done.4), channel_id=1, source_target_pairs={{0,16},{1,3},{2,18},{3,1},{4,20},{5,7},{6,22},{7,5},{8,24},{9,11},... | collective-permute-start | bytes 608264 | tf_op jit(solution)/shard_map/ppermute | solution.py:44
  30.2 1.6 %collective-permute-start.13 = (bf16[32,4224]{1,0:T(8,128)(2,1)S(1)}, bf16[32,4224]{1,0:T(8,128)(2,1)S(1)}, u32[]{:S(2)}, u32[]{:S(2)}) collective-permute-start(bf16[32,4224]{1,0:T(8,128)(2,1)S(1)} %pad_maximum_fusion.1.refs_0_.refs_4_), channel_id=1, source_target_pairs={{0,1},{1,0},{2,3},{3,2},{4,5},{5,4},{6,7},{7,6},{8,9},{9,8},{10,11... | collective-permute-start | bytes 811016 | tf_op jit(solution)/shard_map/ppermute | solution.py:44
  30.2 1.9 %collective-permute-start.14 = (bf16[32,4224]{1,0:T(8,128)(2,1)S(1)}, bf16[32,4224]{1,0:T(8,128)(2,1)S(1)}, u32[]{:S(2)}, u32[]{:S(2)}) collective-permute-start(bf16[32,4224]{1,0:T(8,128)(2,1)S(1)} %pad_maximum_fusion.2.refs_1_.refs_5_), channel_id=1, source_target_pairs={{0,1},{1,0},{2,3},{3,2},{4,5},{5,4},{6,7},{7,6},{8,9},{9,8},{10,11... | collective-permute-start | bytes 811016 | tf_op jit(solution)/shard_map/ppermute | solution.py:44
  35.0 1.6 %collective-permute-start.15 = (bf16[64,2048]{1,0:T(8,128)(2,1)S(1)}, bf16[64,2048]{1,0:T(8,128)(2,1)S(1)}, u32[]{:S(2)}, u32[]{:S(2)}) collective-permute-start(bf16[64,2048]{1,0:T(8,128)(2,1)S(1)} %get-tuple-element.35), channel_id=1, source_target_pairs={{0,1},{1,0},{2,3},{3,2},{4,5},{5,4},{6,7},{7,6},{8,9},{9,8},{10,11... | collective-permute-start | bytes 786440 | tf_op jit(solution)/shard_map/ppermute | solution.py:44
  35.2 2.1 %collective-permute-start.7 = (bf16[64,2048]{1,0:T(8,128)(2,1)S(1)}, bf16[64,2048]{1,0:T(8,128)(2,1)S(1)}, u32[]{:S(2)}, u32[]{:S(2)}) collective-permute-start(bf16[64,2048]{1,0:T(8,128)(2,1)S(1)} %get-tuple-element.30), channel_id=1, source_target_pairs={{0,1},{1,0},{2,3},{3,2},{4,5},{5,4},{6,7},{7,6},{8,9},{9,8},{10,11... | collective-permute-start | bytes 786440 | tf_op jit(solution)/shard_map/ppermute | solution.py:44
  36.7 7.4 %collective-permute-start.16 = (bf16[32,2048]{1,0:T(8,128)(2,1)S(1)}, bf16[32,2048]{1,0:T(8,128)(2,1)S(1)}, u32[]{:S(2)}, u32[]{:S(2)}) collective-permute-start(bf16[32,2048]{1,0:T(8,128)(2,1)S(1)} %get-tuple-element.48), channel_id=1, source_target_pairs={{0,16},{1,3},{2,18},{3,1},{4,20},{5,7},{6,22},{7,5},{8,24},{9,11},... | collective-permute-start | bytes 393224 | tf_op jit(solution)/shard_map/ppermute | solution.py:44
  37.4 6.7 %collective-permute-start.8 = (bf16[32,2048]{1,0:T(8,128)(2,1)S(1)}, bf16[32,2048]{1,0:T(8,128)(2,1)S(1)}, u32[]{:S(2)}, u32[]{:S(2)}) collective-permute-start(bf16[32,2048]{1,0:T(8,128)(2,1)S(1)} %slice.17), channel_id=1, source_target_pairs={{0,2},{1,17},{2,0},{3,19},{4,6},{5,21},{6,4},{7,23},{8,10},{9,25},... | collective-permute-start | bytes 393224 | tf_op jit(solution)/shard_map/ppermute | solution.py:44
  38.9 7.5 %collective-permute-start.17 = (bf16[32,2048]{1,0:T(8,128)(2,1)S(1)}, bf16[32,2048]{1,0:T(8,128)(2,1)S(1)}, u32[]{:S(2)}, u32[]{:S(2)}) collective-permute-start(bf16[32,2048]{1,0:T(8,128)(2,1)S(1)} %get-tuple-element.49), channel_id=1, source_target_pairs={{0,18},{1,19},{2,16},{3,17},{4,22},{5,23},{6,20},{7,21},{8,26},{9,... | collective-permute-start | bytes 393224 | tf_op jit(solution)/shard_map/ppermute | solution.py:44
  46.5 6.8 %collective-permute-start.20 = (bf16[8,2048]{1,0:T(8,128)(2,1)S(1)}, bf16[8,2048]{1,0:T(8,128)(2,1)S(1)}, u32[]{:S(2)}, u32[]{:S(2)}) collective-permute-start(bf16[8,2048]{1,0:T(8,128)(2,1)S(1)} %get-tuple-element.51), channel_id=1, source_target_pairs={{0,12},{1,13},{2,14},{3,15},{4,8},{5,9},{6,10},{7,11},{8,4},{9,5},... | collective-permute-start | bytes 98312 | tf_op jit(solution)/shard_map/ppermute | solution.py:44
  49.0 4.8 %collective-permute-start.19 = (bf16[8,2048]{1,0:T(8,128)(2,1)S(1)}, bf16[8,2048]{1,0:T(8,128)(2,1)S(1)}, u32[]{:S(2)}, u32[]{:S(2)}) collective-permute-start(bf16[8,2048]{1,0:T(8,128)(2,1)S(1)} %get-tuple-element.52), channel_id=1, source_target_pairs={{0,8},{1,9},{2,10},{3,11},{4,12},{5,13},{6,14},{7,15},{8,0},{9,1},... | collective-permute-start | bytes 98312 | tf_op jit(solution)/shard_map/ppermute | solution.py:44
  49.0 4.8 %collective-permute-start.18 = (bf16[8,2048]{1,0:T(8,128)(2,1)S(1)}, bf16[8,2048]{1,0:T(8,128)(2,1)S(1)}, u32[]{:S(2)}, u32[]{:S(2)}) collective-permute-start(bf16[8,2048]{1,0:T(8,128)(2,1)S(1)} %get-tuple-element.50), channel_id=1, source_target_pairs={{0,4},{1,5},{2,6},{3,7},{4,0},{5,1},{6,2},{7,3},{8,12},{9,13},{10,... | collective-permute-start | bytes 98312 | tf_op jit(solution)/shard_map/ppermute | solution.py:44

commit v2 on v1

--- a/solution.py
+++ b/solution.py
@@ -102,18 +102,6 @@
     )(*in_hbm(tokens, out_grad, expert_ids, gate_values))
 
 
-def bring_kernel(count, *refs):
-    sources, targets, copied = refs[:count], refs[count:-1], refs[-1]
-    copies = [
-        pltpu.make_async_copy(source, target, copied.at[i])
-        for i, (source, target) in enumerate(zip(sources, targets))
-    ]
-    for copy in copies:
-        copy.start()
-    for copy in copies:
-        copy.wait()
-
-
 def column_kernel(expert_count, mine):
     column = lax.broadcasted_iota(jnp.int32, mine.shape, 1)
     own = lax.rem(column, expert_count) == lax.axis_index("expert")
@@ -125,21 +113,10 @@
         functools.partial(column_kernel, expert_count),
         out_shape=jax.ShapeDtypeStruct((1, gate_width), jnp.float32),
         out_specs=pl.BlockSpec(memory_space=pltpu.VMEM),
+        cost_estimate=pl.CostEstimate(flops=8 << 30, bytes_accessed=0, transcendentals=0),
         compiler_params=pltpu.CompilerParams(vmem_limit_bytes=1 << 20),
         name="own_columns",
     )()
-
-
-def bring(values):
-    return pl.pallas_call(
-        functools.partial(bring_kernel, len(values)),
-        out_shape=[jax.ShapeDtypeStruct(value.shape, value.dtype) for value in values],
-        in_specs=[pl.BlockSpec(memory_space=pltpu.HBM)] * len(values),
-        out_specs=[pl.BlockSpec(memory_space=pltpu.VMEM)] * len(values),
-        scratch_shapes=[pltpu.SemaphoreType.DMA((len(values),))],
-        compiler_params=pltpu.CompilerParams(vmem_limit_bytes=8 << 20),
-        name="bring",
-    )(*in_hbm(*values))
 
 
 def pass_kernel(piece_count, *refs):
@@ -262,7 +239,7 @@
 
     rows = routed_rows(tokens, out_grad, expert_ids, gate_values, expert_count)
     lines = [rows] + [along(rows, i) for i in range(1, line)]
-    weights = bring((w_gate[0], w_up[0], w_down[0]))
+    weights = (w_gate[0], w_up[0], w_down[0])
     mine = own_columns(expert_count, rows.shape[1] - 2 * model_width)
     join = lambda *values: jnp.concatenate(values, axis=0)
     rest = join(*lines[1:])

time: 54.6 us -> 54.4 us (level)
  Pallas kernels: 15.4 us -> 12.5 us
  waiting for transfers between devices: 14.6 us -> 17.2 us
    pallas_call x1 -> x0, Pallas kernels: 2.88 us -> none  [bring(): pl.pallas_call(functools.partial(bring_kernel, len(values)), out_shape=[j...]
    ppermute x21, waiting for transfers between devices: 14.6 us -> 17.2 us  [swap(): return lax.ppermute(value, AXES, pairs)]
  transfers between devices with their start and end apart: 21 -> 21, of which waited for: 7 -> 9; matrix products, arithmetic and copies ran while one was open for 1% -> 1% of each run, Pallas kernels for 16% -> 11%
where the time goes in v2:
time: 54.4 us; the launch traced here: 54.2 us
  starting transfers between devices  22.6 us (42%)
  waiting for transfers between devices  17.2 us (32%)
  Pallas kernels  12.5 us (23%)
  other arithmetic  0.9 us (2%)
  between operations  0.87 us (2%)
    ppermute x21, starting transfers between devices, swap(): return lax.ppermute(value, AXES, pairs)  22.6 us
    ppermute x21, waiting for transfers between devices, swap(): return lax.ppermute(value, AXES, pairs)  17.2 us
    pallas_call x2, Pallas kernels, outer_sums(): pl.pallas_call(functools.partial(outer_kernel, len(lefts), len(rights), s...  6.04 us
    pallas_call x2, Pallas kernels, expert_pass(): pl.pallas_call(functools.partial(pass_kernel, len(pieces)), out_shape=(hi...  5.63 us
  transfers between devices with their start and end apart: 21, of which 9 were waited for; matrix products, arithmetic and copies ran while one was open for 1% of the time, Pallas kernels for 11%

profile of v2, /device:TPU:0, one launch (start us, length us, event | category | flops | bytes accessed | tf_op | source)
XLA Modules:
  0.0 54.2 jit_solution(12806240537081310063)
XLA Ops:
  0.6 0.8 %routed_rows.1 = bf16[8,4224]{1,0:T(8,128)(2,1)S(1)} custom-call(bf16[8,2048]{1,0:T(8,128)(2,1)} %tokens.1, bf16[8,2048]{1,0:T(8,128)(2,1)} %out_grad.1, s32[8,8]{1,0:T(8,128)} %expert_ids.1, f32[8,8]{1,0:T(8,128)} %gate_values.1), custom_call_target="tpu_custom_call" | custom-call | tf_op jit(solution)/shard_map/routed_rows/pallas_call | solution.py:88
  1.5 3.1 %collective-permute-start = (bf16[8,4224]{1,0:T(8,128)(2,1)S(1)}, bf16[8,4224]{1,0:T(8,128)(2,1)S(1)}, u32[]{:S(2)}, u32[]{:S(2)}) collective-permute-start(bf16[8,4224]{1,0:T(8,128)(2,1)S(1)} %routed_rows.1), channel_id=1, source_target_pairs={{0,4},{1,5},{2,6},{3,7},{4,0},{5,1},{6,2},{7,3},{8,12},{9,13},{10,... | collective-permute-start | bytes 202760 | tf_op jit(solution)/shard_map/ppermute | solution.py:44
  4.6 2.6 %collective-permute-start.1 = (bf16[8,4224]{1,0:T(8,128)(2,1)S(1)}, bf16[8,4224]{1,0:T(8,128)(2,1)S(1)}, u32[]{:S(2)}, u32[]{:S(2)}) collective-permute-start(bf16[8,4224]{1,0:T(8,128)(2,1)S(1)} %routed_rows.1), channel_id=1, source_target_pairs={{0,8},{1,9},{2,10},{3,11},{4,12},{5,13},{6,14},{7,15},{8,0},{9,1},... | collective-permute-start | bytes 202760 | tf_op jit(solution)/shard_map/ppermute | solution.py:44
  7.2 1.7 %collective-permute-start.9 = (bf16[8,4224]{1,0:T(8,128)(2,1)S(1)}, bf16[8,4224]{1,0:T(8,128)(2,1)S(1)}, u32[]{:S(2)}, u32[]{:S(2)}) collective-permute-start(bf16[8,4224]{1,0:T(8,128)(2,1)S(1)} %routed_rows.1), channel_id=1, source_target_pairs={{0,16},{1,3},{2,18},{3,1},{4,20},{5,7},{6,22},{7,5},{8,24},{9,11},... | collective-permute-start | bytes 202760 | tf_op jit(solution)/shard_map/ppermute | solution.py:44
  8.9 1.5 %collective-permute-start.3 = (bf16[8,4224]{1,0:T(8,128)(2,1)S(1)}, bf16[8,4224]{1,0:T(8,128)(2,1)S(1)}, u32[]{:S(2)}, u32[]{:S(2)}) collective-permute-start(bf16[8,4224]{1,0:T(8,128)(2,1)S(1)} %routed_rows.1), channel_id=1, source_target_pairs={{0,2},{1,17},{2,0},{3,19},{4,6},{5,21},{6,4},{7,23},{8,10},{9,25},... | collective-permute-start | bytes 202760 | tf_op jit(solution)/shard_map/ppermute | solution.py:44
  10.5 1.5 %collective-permute-done.1 = bf16[8,4224]{1,0:T(8,128)(2,1)S(1)} collective-permute-done((bf16[8,4224]{1,0:T(8,128)(2,1)S(1)}, bf16[8,4224]{1,0:T(8,128)(2,1)S(1)}, u32[]{:S(2)}, u32[]{:S(2)}) %collective-permute-start.1) | collective-permute-done | bytes 67616 | tf_op jit(solution)/shard_map/ppermute | solution.py:44
  12.0 1.4 %collective-permute-done.2 = bf16[8,4224]{1,0:T(8,128)(2,1)S(1)} collective-permute-done((bf16[8,4224]{1,0:T(8,128)(2,1)S(1)}, bf16[8,4224]{1,0:T(8,128)(2,1)S(1)}, u32[]{:S(2)}, u32[]{:S(2)}) %collective-permute-start.2) | collective-permute-done | bytes 67616 | tf_op jit(solution)/shard_map/ppermute | solution.py:44
  13.4 1.5 %collective-permute-start.10 = (bf16[24,4224]{1,0:T(8,128)(2,1)S(1)}, bf16[24,4224]{1,0:T(8,128)(2,1)S(1)}, u32[]{:S(2)}, u32[]{:S(2)}) collective-permute-start(bf16[24,4224]{1,0:T(8,128)(2,1)S(1)} %constant_dynamic-update-slice_fusion), channel_id=1, source_target_pairs={{0,16},{1,3},{2,18},{3,1},{4,20},{5,7},{6,22},{7,5},{8,24},{9,11},... | collective-permute-start | bytes 608264 | tf_op jit(solution)/shard_map/ppermute | solution.py:44
  15.0 1.5 %collective-permute-start.4 = (bf16[24,4224]{1,0:T(8,128)(2,1)S(1)}, bf16[24,4224]{1,0:T(8,128)(2,1)S(1)}, u32[]{:S(2)}, u32[]{:S(2)}) collective-permute-start(bf16[24,4224]{1,0:T(8,128)(2,1)S(1)} %constant_dynamic-update-slice_fusion), channel_id=1, source_target_pairs={{0,2},{1,17},{2,0},{3,19},{4,6},{5,21},{6,4},{7,23},{8,10},{9,25},... | collective-permute-start | bytes 608264 | tf_op jit(solution)/shard_map/ppermute | solution.py:44
  17.2 4.2 %collective-permute-done.4 = bf16[24,4224]{1,0:T(8,128)(2,1)S(1)} collective-permute-done((bf16[24,4224]{1,0:T(8,128)(2,1)S(1)}, bf16[24,4224]{1,0:T(8,128)(2,1)S(1)}, u32[]{:S(2)}, u32[]{:S(2)}) %collective-permute-start.4) | collective-permute-done | bytes 202784 | tf_op jit(solution)/shard_map/ppermute | solution.py:44
  22.2 5.2 %collective-permute-done.12 = bf16[24,4224]{1,0:T(8,128)(2,1)S(1)} collective-permute-done((bf16[24,4224]{1,0:T(8,128)(2,1)S(1)}, bf16[24,4224]{1,0:T(8,128)(2,1)S(1)}, u32[]{:S(2)}, u32[]{:S(2)}) %collective-permute-start.12) | collective-permute-done | bytes 202784 | tf_op jit(solution)/shard_map/ppermute | solution.py:44
  27.4 2.8 %shard_map.102 = (bf16[128,512]{1,0:T(8,128)(2,1)S(1)}, bf16[128,512]{1,0:T(8,128)(2,1)S(1)}, bf16[128,512]{1,0:T(8,128)(2,1)S(1)}, bf16[128,2048]{1,0:T(8,128)(...) custom-call(bf16[32,4224]{1,0:T(8,128)(2,1)S(1)} %pad_maximum_fusion.refs_0_, ...), custom_call_target="tpu_custom_call" | custom-call | flops 1342177280 | bytes 6291456 | tf_op jit(solution)/shard_map/pallas_call | solution.py:159
  30.8 1.0 %collective-permute-done.13.refs_2_.refs_6_ = bf16[32,4224]{1,0:T(8,128)(2,1)S(1)} collective-permute-done((bf16[32,4224]{1,0:T(8,128)(2,1)S(1)}, bf16[32,4224]{1,0:T(8,128)(2,1)S(1)}, u32[]{:S(2)}, u32[]{:S(2)}) %collective-permute-start.13) | collective-permute-done | bytes 270368 | tf_op jit(solution)/shard_map/ppermute | solution.py:44
  32.2 2.8 %shard_map.103 = (bf16[128,512]{1,0:T(8,128)(2,1)S(1)}, bf16[128,512]{1,0:T(8,128)(2,1)S(1)}, bf16[128,512]{1,0:T(8,128)(2,1)S(1)}, bf16[128,2048]{1,0:T(8,128)(...) custom-call(bf16[32,4224]{1,0:T(8,128)(2,1)S(1)} %pad_maximum_fusion.1.refs_0_.refs_4_, ...), custom_call_target="tpu_custom_call" | custom-call | flops 1342177280 | bytes 6291456 | tf_op jit(solution)/shard_map/pallas_call | solution.py:159
  35.6 1.0 %collective-permute-done.15 = bf16[64,2048]{1,0:T(8,128)(2,1)S(1)} collective-permute-done((bf16[64,2048]{1,0:T(8,128)(2,1)S(1)}, bf16[64,2048]{1,0:T(8,128)(2,1)S(1)}, u32[]{:S(2)}, u32[]{:S(2)}) %collective-permute-start.15) | collective-permute-done | bytes 262176 | tf_op jit(solution)/shard_map/ppermute | solution.py:44
  36.8 0.6 %collective-permute-start.16 = (bf16[32,2048]{1,0:T(8,128)(2,1)S(1)}, bf16[32,2048]{1,0:T(8,128)(2,1)S(1)}, u32[]{:S(2)}, u32[]{:S(2)}) collective-permute-start(bf16[32,2048]{1,0:T(8,128)(2,1)S(1)} %get-tuple-element.42), channel_id=1, source_target_pairs={{0,16},{1,3},{2,18},{3,1},{4,20},{5,7},{6,22},{7,5},{8,24},{9,11},... | collective-permute-start | bytes 393224 | tf_op jit(solution)/shard_map/ppermute | solution.py:44
  37.5 1.6 %collective-permute-start.8 = (bf16[32,2048]{1,0:T(8,128)(2,1)S(1)}, bf16[32,2048]{1,0:T(8,128)(2,1)S(1)}, u32[]{:S(2)}, u32[]{:S(2)}) collective-permute-start(bf16[32,2048]{1,0:T(8,128)(2,1)S(1)} %slice.17), channel_id=1, source_target_pairs={{0,2},{1,17},{2,0},{3,19},{4,6},{5,21},{6,4},{7,23},{8,10},{9,25},... | collective-permute-start | bytes 393224 | tf_op jit(solution)/shard_map/ppermute | solution.py:44
  39.0 1.4 %collective-permute-start.17 = (bf16[32,2048]{1,0:T(8,128)(2,1)S(1)}, bf16[32,2048]{1,0:T(8,128)(2,1)S(1)}, u32[]{:S(2)}, u32[]{:S(2)}) collective-permute-start(bf16[32,2048]{1,0:T(8,128)(2,1)S(1)} %get-tuple-element.43), channel_id=1, source_target_pairs={{0,18},{1,19},{2,16},{3,17},{4,22},{5,23},{6,20},{7,21},{8,26},{9,... | collective-permute-start | bytes 393224 | tf_op jit(solution)/shard_map/ppermute | solution.py:44
  40.5 3.7 %shard_map.104 = (f32[2048,512]{1,0:T(8,128)}, f32[2048,512]{1,0:T(8,128)}) custom-call(bf16[32,4224]{1,0:T(8,128)(2,1)S(1)} %pad_maximum_fusion.refs_0_, bf16[32,4224]{1,0:T(8,128)(2,1)S(1)} %constant_dynamic-update-slice_fusion.3.refs_1_, bf16[32,4224]{1,0:T(8,128)(2,1)S(1)} %collective-permute-done.5.refs_2_, ...), custom_call_target="tpu_custom_call" | custom-call | flops 1073741824 | bytes 8388608 | tf_op jit(solution)/shard_map/pallas_call | solution.py:201
  44.2 2.3 %collective-permute-done.17 = bf16[32,2048]{1,0:T(8,128)(2,1)S(1)} collective-permute-done((bf16[32,2048]{1,0:T(8,128)(2,1)S(1)}, bf16[32,2048]{1,0:T(8,128)(2,1)S(1)}, u32[]{:S(2)}, u32[]{:S(2)}) %collective-permute-start.17) | collective-permute-done | bytes 131104 | tf_op jit(solution)/shard_map/ppermute | solution.py:44
  46.6 1.9 %collective-permute-start.20 = (bf16[8,2048]{1,0:T(8,128)(2,1)S(1)}, bf16[8,2048]{1,0:T(8,128)(2,1)S(1)}, u32[]{:S(2)}, u32[]{:S(2)}) collective-permute-start(bf16[8,2048]{1,0:T(8,128)(2,1)S(1)} %get-tuple-element.45), channel_id=1, source_target_pairs={{0,12},{1,13},{2,14},{3,15},{4,8},{5,9},{6,10},{7,11},{8,4},{9,5},... | collective-permute-start | bytes 98312 | tf_op jit(solution)/shard_map/ppermute | solution.py:44
  48.8 2.3 %collective-permute-start.18 = (bf16[8,2048]{1,0:T(8,128)(2,1)S(1)}, bf16[8,2048]{1,0:T(8,128)(2,1)S(1)}, u32[]{:S(2)}, u32[]{:S(2)}) collective-permute-start(bf16[8,2048]{1,0:T(8,128)(2,1)S(1)} %get-tuple-element.44), channel_id=1, source_target_pairs={{0,4},{1,5},{2,6},{3,7},{4,0},{5,1},{6,2},{7,3},{8,12},{9,13},{10,... | collective-permute-start | bytes 98312 | tf_op jit(solution)/shard_map/ppermute | solution.py:44
  51.1 2.4 %shard_map.105 = f32[512,2048]{1,0:T(8,128)} custom-call(bf16[128,512]{1,0:T(8,128)(2,1)S(1)} %get-tuple-element.25.refs_0_, bf16[128,512]{1,0:T(8,128)(2,1)S(1)} %get-tuple-element.39.refs_1_, bf16[128,2048]{1,0:T(8,128)(2,1)S(1)} %get-tuple-element.40.refs_2_, bf16[128,2048]{1,0:T(8,128)(2,1)S(1)} %get-tuple-element.41.refs_3_), custom_call_target="tpu_custom_call" | custom-call | flops 536870912 | bytes 4194304 | tf_op jit(solution)/shard_map/pallas_call | solution.py:201
  53.6 0.6 %add_convert_fusion.3 = bf16[8,2048]{1,0:T(8,128)(2,1)} fusion(bf16[8,2048]{1,0:T(8,128)(2,1)S(1)} %collective-permute-done.20, bf16[8,2048]{1,0:T(8,128)(2,1)S(1)} %collective-permute-done.19, bf16[8,2048]{1,0:T(8,128)(2,1)S(1)} %collective-permute-done.18, bf16[32,2048]{1,0:T(8,128)(2,1)S(1)} %add_convert_fusion.2), kind=kLoop, calls=%fused_computation.6 | loop fusion | flops 131072 | bytes 163840 | tf_op jit(solution)/shard_map/convert_element_type | solution.py:218
  (45 shorter events, 3.7 us)
Async XLA Ops:
  1.5 25.9 %copy-start = (bf16[1,2048,512]{2,1,0:T(8,128)(2,1)S(1)}, bf16[1,2048,512]{2,1,0:T(8,128)(2,1)}, u32[]{:S(2)}) copy-start(bf16[1,2048,512]{2,1,0:T(8,128)(2,1)} %param.11) | copy-start | bytes 6291460
  1.5 25.9 %copy-start.1 = (bf16[1,2048,512]{2,1,0:T(8,128)(2,1)S(1)}, bf16[1,2048,512]{2,1,0:T(8,128)(2,1)}, u32[]{:S(2)}) copy-start(bf16[1,2048,512]{2,1,0:T(8,128)(2,1)} %param.12) | copy-start | bytes 6291460
  1.5 25.9 %copy-start.2 = (bf16[1,512,2048]{2,1,0:T(8,128)(2,1)S(1)}, bf16[1,512,2048]{2,1,0:T(8,128)(2,1)}, u32[]{:S(2)}) copy-start(bf16[1,512,2048]{2,1,0:T(8,128)(2,1)} %param.13) | copy-start | bytes 6291460
  1.5 8.9 %collective-permute-start = (bf16[8,4224]{1,0:T(8,128)(2,1)S(1)}, bf16[8,4224]{1,0:T(8,128)(2,1)S(1)}, u32[]{:S(2)}, u32[]{:S(2)}) collective-permute-start(bf16[8,4224]{1,0:T(8,128)(2,1)S(1)} %routed_rows.1), channel_id=1, source_target_pairs={{0,4},{1,5},{2,6},{3,7},{4,0},{5,1},{6,2},{7,3},{8,12},{9,13},{10,... | collective-permute-start | bytes 202760 | tf_op jit(solution)/shard_map/ppermute | solution.py:44
  4.6 7.4 %collective-permute-start.1 = (bf16[8,4224]{1,0:T(8,128)(2,1)S(1)}, bf16[8,4224]{1,0:T(8,128)(2,1)S(1)}, u32[]{:S(2)}, u32[]{:S(2)}) collective-permute-start(bf16[8,4224]{1,0:T(8,128)(2,1)S(1)} %routed_rows.1), channel_id=1, source_target_pairs={{0,8},{1,9},{2,10},{3,11},{4,12},{5,13},{6,14},{7,15},{8,0},{9,1},... | collective-permute-start | bytes 202760 | tf_op jit(solution)/shard_map/ppermute | solution.py:44
  7.2 6.2 %collective-permute-start.2 = (bf16[8,4224]{1,0:T(8,128)(2,1)S(1)}, bf16[8,4224]{1,0:T(8,128)(2,1)S(1)}, u32[]{:S(2)}, u32[]{:S(2)}) collective-permute-start(bf16[8,4224]{1,0:T(8,128)(2,1)S(1)} %routed_rows.1), channel_id=1, source_target_pairs={{0,12},{1,13},{2,14},{3,15},{4,8},{5,9},{6,10},{7,11},{8,4},{9,5},... | collective-permute-start | bytes 202760 | tf_op jit(solution)/shard_map/ppermute | solution.py:44
  7.2 14.3 %collective-permute-start.9 = (bf16[8,4224]{1,0:T(8,128)(2,1)S(1)}, bf16[8,4224]{1,0:T(8,128)(2,1)S(1)}, u32[]{:S(2)}, u32[]{:S(2)}) collective-permute-start(bf16[8,4224]{1,0:T(8,128)(2,1)S(1)} %routed_rows.1), channel_id=1, source_target_pairs={{0,16},{1,3},{2,18},{3,1},{4,20},{5,7},{6,22},{7,5},{8,24},{9,11},... | collective-permute-start | bytes 202760 | tf_op jit(solution)/shard_map/ppermute | solution.py:44
  8.9 7.7 %collective-permute-start.3 = (bf16[8,4224]{1,0:T(8,128)(2,1)S(1)}, bf16[8,4224]{1,0:T(8,128)(2,1)S(1)}, u32[]{:S(2)}, u32[]{:S(2)}) collective-permute-start(bf16[8,4224]{1,0:T(8,128)(2,1)S(1)} %routed_rows.1), channel_id=1, source_target_pairs={{0,2},{1,17},{2,0},{3,19},{4,6},{5,21},{6,4},{7,23},{8,10},{9,25},... | collective-permute-start | bytes 202760 | tf_op jit(solution)/shard_map/ppermute | solution.py:44
  13.4 8.7 %collective-permute-start.10 = (bf16[24,4224]{1,0:T(8,128)(2,1)S(1)}, bf16[24,4224]{1,0:T(8,128)(2,1)S(1)}, u32[]{:S(2)}, u32[]{:S(2)}) collective-permute-start(bf16[24,4224]{1,0:T(8,128)(2,1)S(1)} %constant_dynamic-update-slice_fusion), channel_id=1, source_target_pairs={{0,16},{1,3},{2,18},{3,1},{4,20},{5,7},{6,22},{7,5},{8,24},{9,11},... | collective-permute-start | bytes 608264 | tf_op jit(solution)/shard_map/ppermute | solution.py:44
  15.0 6.5 %collective-permute-start.4 = (bf16[24,4224]{1,0:T(8,128)(2,1)S(1)}, bf16[24,4224]{1,0:T(8,128)(2,1)S(1)}, u32[]{:S(2)}, u32[]{:S(2)}) collective-permute-start(bf16[24,4224]{1,0:T(8,128)(2,1)S(1)} %constant_dynamic-update-slice_fusion), channel_id=1, source_target_pairs={{0,2},{1,17},{2,0},{3,19},{4,6},{5,21},{6,4},{7,23},{8,10},{9,25},... | collective-permute-start | bytes 608264 | tf_op jit(solution)/shard_map/ppermute | solution.py:44
  16.5 10.8 %collective-permute-start.5 = (bf16[32,4224]{1,0:T(8,128)(2,1)S(1)}, bf16[32,4224]{1,0:T(8,128)(2,1)S(1)}, u32[]{:S(2)}, u32[]{:S(2)}) collective-permute-start(bf16[32,4224]{1,0:T(8,128)(2,1)S(1)} %pad_maximum_fusion.refs_0_), channel_id=1, source_target_pairs={{0,1},{1,0},{2,3},{3,2},{4,5},{5,4},{6,7},{7,6},{8,9},{9,8},{10,11... | collective-permute-start | bytes 811016 | tf_op jit(solution)/shard_map/ppermute | solution.py:44
  16.6 5.6 %collective-permute-start.11 = (bf16[8,4224]{1,0:T(8,128)(2,1)S(1)}, bf16[8,4224]{1,0:T(8,128)(2,1)S(1)}, u32[]{:S(2)}, u32[]{:S(2)}) collective-permute-start(bf16[8,4224]{1,0:T(8,128)(2,1)S(1)} %collective-permute-done.3), channel_id=1, source_target_pairs={{0,16},{1,3},{2,18},{3,1},{4,20},{5,7},{6,22},{7,5},{8,24},{9,11},... | collective-permute-start | bytes 202760 | tf_op jit(solution)/shard_map/ppermute | solution.py:44
  21.5 5.9 %collective-permute-start.6 = (bf16[32,4224]{1,0:T(8,128)(2,1)S(1)}, bf16[32,4224]{1,0:T(8,128)(2,1)S(1)}, u32[]{:S(2)}, u32[]{:S(2)}) collective-permute-start(bf16[32,4224]{1,0:T(8,128)(2,1)S(1)} %constant_dynamic-update-slice_fusion.3.refs_1_), channel_id=1, source_target_pairs={{0,1},{1,0},{2,3},{3,2},{4,5},{5,4},{6,7},{7,6},{8,9},{9,8},{10,11... | collective-permute-start | bytes 811016 | tf_op jit(solution)/shard_map/ppermute | solution.py:44
  21.5 5.8 %collective-permute-start.12 = (bf16[24,4224]{1,0:T(8,128)(2,1)S(1)}, bf16[24,4224]{1,0:T(8,128)(2,1)S(1)}, u32[]{:S(2)}, u32[]{:S(2)}) collective-permute-start(bf16[24,4224]{1,0:T(8,128)(2,1)S(1)} %collective-permute-done.4), channel_id=1, source_target_pairs={{0,16},{1,3},{2,18},{3,1},{4,20},{5,7},{6,22},{7,5},{8,24},{9,11},... | collective-permute-start | bytes 608264 | tf_op jit(solution)/shard_map/ppermute | solution.py:44
  30.2 1.6 %collective-permute-start.13 = (bf16[32,4224]{1,0:T(8,128)(2,1)S(1)}, bf16[32,4224]{1,0:T(8,128)(2,1)S(1)}, u32[]{:S(2)}, u32[]{:S(2)}) collective-permute-start(bf16[32,4224]{1,0:T(8,128)(2,1)S(1)} %pad_maximum_fusion.1.refs_0_.refs_4_), channel_id=1, source_target_pairs={{0,1},{1,0},{2,3},{3,2},{4,5},{5,4},{6,7},{7,6},{8,9},{9,8},{10,11... | collective-permute-start | bytes 811016 | tf_op jit(solution)/shard_map/ppermute | solution.py:44
  30.3 1.9 %collective-permute-start.14 = (bf16[32,4224]{1,0:T(8,128)(2,1)S(1)}, bf16[32,4224]{1,0:T(8,128)(2,1)S(1)}, u32[]{:S(2)}, u32[]{:S(2)}) collective-permute-start(bf16[32,4224]{1,0:T(8,128)(2,1)S(1)} %pad_maximum_fusion.2.refs_1_.refs_5_), channel_id=1, source_target_pairs={{0,1},{1,0},{2,3},{3,2},{4,5},{5,4},{6,7},{7,6},{8,9},{9,8},{10,11... | collective-permute-start | bytes 811016 | tf_op jit(solution)/shard_map/ppermute | solution.py:44
  35.1 1.6 %collective-permute-start.15 = (bf16[64,2048]{1,0:T(8,128)(2,1)S(1)}, bf16[64,2048]{1,0:T(8,128)(2,1)S(1)}, u32[]{:S(2)}, u32[]{:S(2)}) collective-permute-start(bf16[64,2048]{1,0:T(8,128)(2,1)S(1)} %get-tuple-element.29), channel_id=1, source_target_pairs={{0,1},{1,0},{2,3},{3,2},{4,5},{5,4},{6,7},{7,6},{8,9},{9,8},{10,11... | collective-permute-start | bytes 786440 | tf_op jit(solution)/shard_map/ppermute | solution.py:44
  35.3 2.1 %collective-permute-start.7 = (bf16[64,2048]{1,0:T(8,128)(2,1)S(1)}, bf16[64,2048]{1,0:T(8,128)(2,1)S(1)}, u32[]{:S(2)}, u32[]{:S(2)}) collective-permute-start(bf16[64,2048]{1,0:T(8,128)(2,1)S(1)} %get-tuple-element.24), channel_id=1, source_target_pairs={{0,1},{1,0},{2,3},{3,2},{4,5},{5,4},{6,7},{7,6},{8,9},{9,8},{10,11... | collective-permute-start | bytes 786440 | tf_op jit(solution)/shard_map/ppermute | solution.py:44
  36.8 7.4 %collective-permute-start.16 = (bf16[32,2048]{1,0:T(8,128)(2,1)S(1)}, bf16[32,2048]{1,0:T(8,128)(2,1)S(1)}, u32[]{:S(2)}, u32[]{:S(2)}) collective-permute-start(bf16[32,2048]{1,0:T(8,128)(2,1)S(1)} %get-tuple-element.42), channel_id=1, source_target_pairs={{0,16},{1,3},{2,18},{3,1},{4,20},{5,7},{6,22},{7,5},{8,24},{9,11},... | collective-permute-start | bytes 393224 | tf_op jit(solution)/shard_map/ppermute | solution.py:44
  37.5 6.7 %collective-permute-start.8 = (bf16[32,2048]{1,0:T(8,128)(2,1)S(1)}, bf16[32,2048]{1,0:T(8,128)(2,1)S(1)}, u32[]{:S(2)}, u32[]{:S(2)}) collective-permute-start(bf16[32,2048]{1,0:T(8,128)(2,1)S(1)} %slice.17), channel_id=1, source_target_pairs={{0,2},{1,17},{2,0},{3,19},{4,6},{5,21},{6,4},{7,23},{8,10},{9,25},... | collective-permute-start | bytes 393224 | tf_op jit(solution)/shard_map/ppermute | solution.py:44
  39.0 7.5 %collective-permute-start.17 = (bf16[32,2048]{1,0:T(8,128)(2,1)S(1)}, bf16[32,2048]{1,0:T(8,128)(2,1)S(1)}, u32[]{:S(2)}, u32[]{:S(2)}) collective-permute-start(bf16[32,2048]{1,0:T(8,128)(2,1)S(1)} %get-tuple-element.43), channel_id=1, source_target_pairs={{0,18},{1,19},{2,16},{3,17},{4,22},{5,23},{6,20},{7,21},{8,26},{9,... | collective-permute-start | bytes 393224 | tf_op jit(solution)/shard_map/ppermute | solution.py:44
  46.6 6.8 %collective-permute-start.20 = (bf16[8,2048]{1,0:T(8,128)(2,1)S(1)}, bf16[8,2048]{1,0:T(8,128)(2,1)S(1)}, u32[]{:S(2)}, u32[]{:S(2)}) collective-permute-start(bf16[8,2048]{1,0:T(8,128)(2,1)S(1)} %get-tuple-element.45), channel_id=1, source_target_pairs={{0,12},{1,13},{2,14},{3,15},{4,8},{5,9},{6,10},{7,11},{8,4},{9,5},... | collective-permute-start | bytes 98312 | tf_op jit(solution)/shard_map/ppermute | solution.py:44
  48.5 5.1 %collective-permute-start.19 = (bf16[8,2048]{1,0:T(8,128)(2,1)S(1)}, bf16[8,2048]{1,0:T(8,128)(2,1)S(1)}, u32[]{:S(2)}, u32[]{:S(2)}) collective-permute-start(bf16[8,2048]{1,0:T(8,128)(2,1)S(1)} %get-tuple-element.46), channel_id=1, source_target_pairs={{0,8},{1,9},{2,10},{3,11},{4,12},{5,13},{6,14},{7,15},{8,0},{9,1},... | collective-permute-start | bytes 98312 | tf_op jit(solution)/shard_map/ppermute | solution.py:44
  48.8 4.8 %collective-permute-start.18 = (bf16[8,2048]{1,0:T(8,128)(2,1)S(1)}, bf16[8,2048]{1,0:T(8,128)(2,1)S(1)}, u32[]{:S(2)}, u32[]{:S(2)}) collective-permute-start(bf16[8,2048]{1,0:T(8,128)(2,1)S(1)} %get-tuple-element.44), channel_id=1, source_target_pairs={{0,4},{1,5},{2,6},{3,7},{4,0},{5,1},{6,2},{7,3},{8,12},{9,13},{10,... | collective-permute-start | bytes 98312 | tf_op jit(solution)/shard_map/ppermute | solution.py:44
